TPU v7x, 128 devices: a whole 4x4x4 slice. The times are simulated.
128 devices in a mesh: section: 8 (over z, core), expert: 16 (over y, x).
Axes of the slice: x: 4, y: 4, z: 4, core: 2. Of those that a mesh axis runs over, the one named last changes fastest.
Arguments:
- tokens_in: bfloat16 [2, 2048, 1024], P(None, 'expert'), may hold values from -6 to 6
- ln_gain: float32 [8, 1024], P('section'), may hold values from 0.1 to 1.9
- router: bfloat16 [8, 1024, 32], P('section'), may hold values from -0.1875 to 0.1875
- dense_in: bfloat16 [8, 1024, 2048], P('section'), may hold values from -0.1875 to 0.1875
- dense_out: bfloat16 [8, 2048, 1024], P('section'), may hold values from -0.125 to 0.125
- expert_in: bfloat16 [8, 32, 1024, 2048], P('section', 'expert'), may hold values from -0.1875 to 0.1875
- expert_out: bfloat16 [8, 32, 2048, 1024], P('section', 'expert'), may hold values from -0.125 to 0.125
- routes: int32 [8, 2, 2048, 1], P('section', None, 'expert'), may hold values from 0 to 31; in each aligned block of 64 rows (0 to 63, 64 to 127, ..., all dimensions but the last counted through in order) at most 4 rows name the same one
Outputs:
- tokens_out: bfloat16 [2, 2048, 1024], P(None, 'expert', 'section')
Inputs may be any that keep to these rules, and one draw needn't show every extreme that they name: Split every row of 2048 tokens of routes into aligned blocks of 64 tokens. In no block does one id occur more than 4 times, and in every draw some id occurs exactly 4 times in some block.
All inputs are finite; a program needn't handle non-finite values.
Results may differ from a plain program's by a relative error of at most 0.019.
Values may be sent and summed in bfloat16 or wider, within the bound.
No kernel may reach another device: no remote copies, remote signals or barrier semaphores. Data moves between devices by JAX's collectives and lax.ppermute only.
A program may use at most 128 MiB of HBM per device.

v0:
```python
import functools

import jax
import jax.numpy as jnp
from jax import lax
from jax.experimental import pallas as pl
from jax.experimental.pallas import tpu as pltpu
from jax.sharding import PartitionSpec as P

BF16 = jnp.bfloat16
F32 = jnp.float32
VMEM_SPEC = pl.BlockSpec(memory_space=pltpu.VMEM)
LIMIT = 30 << 20
TURNS = 8


def dot(a, b):
    return jnp.dot(a, b, preferred_element_type=F32)


def dot_t(a, b):
    return lax.dot_general(a, b, (((1,), (1,)), ((), ())), preferred_element_type=F32)


def tables_kernel(blocks, routes_ref, gain_ref, *refs):
    tokens_ref = refs[0] if len(refs) == 9 else None
    send_ref, take_ref, picked_ref, held_gain_ref = refs[1:5] if tokens_ref is not None else refs[:4]
    ids_ref, sems = refs[-2:]
    tokens = ids_ref.shape[1]
    moves = [(routes_ref, ids_ref), (gain_ref, held_gain_ref)]
    if tokens_ref is not None:
        moves += [(tokens_ref.at[0], refs[5]), (tokens_ref.at[1], refs[6])]
    copies = [
        pltpu.make_async_copy(source, target, sems.at[number])
        for number, (source, target) in enumerate(moves)
    ]
    for copy in copies:
        copy.start()
    copies[0].wait()
    slots = send_ref.shape[1]
    labels = picked_ref.shape[2]
    earlier = (
        lax.broadcasted_iota(jnp.int32, (tokens, tokens), 0)
        < lax.broadcasted_iota(jnp.int32, (tokens, tokens), 1)
    ).astype(BF16)
    capacity = slots // (labels // 4)
    for block in range(blocks):
        ids = ids_ref[block : block + 1, :]
        picked = (lax.broadcasted_iota(jnp.int32, (labels, tokens), 0) == ids).astype(F32)
        before = dot(picked.astype(BF16), earlier)
        position = jnp.sum(before * picked, axis=0, keepdims=True).astype(jnp.int32)
        slot = ids * capacity + position
        send = (lax.broadcasted_iota(jnp.int32, (slots, tokens), 0) == slot).astype(F32)
        send_ref[block] = send.astype(BF16)
        take_ref[block] = send.T.astype(BF16)
        picked_ref[block] = picked.T
    for copy in copies[1:]:
        copy.wait()


def of_block(pick_ref, table_ref):
    rows, lanes = table_ref.shape[1:]
    second = jnp.broadcast_to(pick_ref[:1, :1] == 1, (rows, lanes))
    return jnp.where(second, table_ref[1].astype(F32), table_ref[0].astype(F32))


def enter_kernel(pick_ref, received_ref, gain_ref, send_ref, normed_ref, outgoing_ref):
    stream = received_ref[...].astype(F32)
    centred = stream - jnp.mean(stream, axis=-1, keepdims=True)
    variance = jnp.mean(centred * centred, axis=-1, keepdims=True)
    normed = (centred * lax.rsqrt(variance + 1e-05) * gain_ref[...]).astype(BF16)
    normed_ref[...] = normed
    outgoing_ref[...] = dot(of_block(pick_ref, send_ref).astype(BF16), normed).astype(BF16)


def mlp(token_rows, weight_in, weight_out):
    activation = jax.nn.gelu(dot(token_rows, weight_in), approximate=True).astype(BF16)
    return dot(activation, weight_out)


def layer_kernel(
    pick_ref,
    received_ref,
    normed_ref,
    incoming_ref,
    picked_ref,
    router_ref,
    dense_in_ref,
    dense_out_ref,
    expert_in_ref,
    expert_out_ref,
    result_ref,
    base_ref,
    gate_ref,
):
    sources, rows, model_width = incoming_ref.shape
    half = rows // 2
    late = (lax.axis_index("section") >= lax.axis_size("section") // 2).astype(jnp.int32)
    normed = normed_ref[...]
    logits = dot_t(normed, router_ref[...])
    picked = of_block(pick_ref, picked_ref)[:, : logits.shape[1]]
    logit = jnp.sum(picked * logits, axis=1, keepdims=True)
    gate_ref[...] = jnp.broadcast_to(jax.nn.sigmoid(logit), gate_ref.shape)
    dense_part = mlp(normed, dense_in_ref[...], dense_out_ref[...])
    base_ref[...] = received_ref[...].astype(F32) + dense_part
    for which, held in ((0, 0), (1, late)):
        window = pl.ds(which * half, half)
        token_rows = incoming_ref[:, window, :].reshape(sources * half, model_width)
        found = mlp(token_rows, expert_in_ref[held], expert_out_ref[held]).astype(BF16)
        result_ref[:, window, :] = found.reshape(sources, half, model_width)


def stream_after(pick_ref, base_ref, gate_ref, take_ref, returned_ref):
    routed = dot(of_block(pick_ref, take_ref).astype(BF16), returned_ref[...])
    return (base_ref[...] + gate_ref[:, :1] * routed).astype(BF16)


def leave_kernel(pick_ref, base_ref, gate_ref, take_ref, returned_ref, stream_ref):
    stream_ref[...] = stream_after(pick_ref, base_ref, gate_ref, take_ref, returned_ref)


def put_shares(stream, out_ref):
    share = out_ref.shape[2]
    for number in range(out_ref.shape[0]):
        out_ref[number] = stream[:, number * share : (number + 1) * share]


def finish_kernel(pick_ref, base_ref, gate_ref, take_ref, returned_ref, out_ref):
    put_shares(stream_after(pick_ref, base_ref, gate_ref, take_ref, returned_ref), out_ref)


def split_kernel(stream_ref, out_ref):
    put_shares(stream_ref[...], out_ref)


def gather_kernel(pieces_ref, out_ref):
    out_ref[0] = pieces_ref[0]
    out_ref[1] = pieces_ref[pieces_ref.shape[0] - 1]


def untouched_kernel(*refs):
    pass


def wait_kernel(turns, source_ref, target_ref, sems):
    rows = source_ref.shape[0] // turns

    def turn(number, _):
        window = pl.ds(pl.multiple_of(number * rows, rows), rows)
        copy = pltpu.make_async_copy(source_ref.at[window], target_ref.at[window], sems.at[0])
        copy.start()
        copy.wait()
        return 0

    lax.fori_loop(0, turns, turn, 0)


def copy_over_kernel(*refs):
    count = len(refs) // 2
    sems = refs[-1]

    @pl.when(lax.axis_index("section") >= 2)
    def _():
        copies = [
            pltpu.make_async_copy(refs[n], refs[count + n], sems.at[n]) for n in range(count)
        ]
        for copy in copies:
            copy.start()
        for copy in copies:
            copy.wait()


def in_hbm(value):
    return pltpu.with_memory_space_constraint(value, pltpu.HBM)


def keep_kernel(source_ref, target_ref):
    target_ref[...] = source_ref[...]


def shape(dims, dtype):
    return jax.ShapeDtypeStruct(dims, dtype)


def kernel_call(kernel, inputs, outputs, cost=None):
    several = isinstance(outputs, tuple)
    return pl.pallas_call(
        kernel,
        out_shape=outputs,
        in_specs=[VMEM_SPEC] * inputs,
        out_specs=[VMEM_SPEC] * len(outputs) if several else VMEM_SPEC,
        cost_estimate=cost,
        compiler_params=pltpu.CompilerParams(vmem_limit_bytes=LIMIT),
    )


def body(tokens_in, ln_gain, router, dense_in, dense_out, expert_in, expert_out, routes):
    sections = lax.axis_size("section")
    members = lax.axis_size("expert")
    section_index = lax.axis_index("section")
    blocks, tok_dev, model_width = tokens_in.shape
    labels = router.shape[2]
    hidden_width = dense_in.shape[2]
    capacity = 2 * (tok_dev // labels)
    slots = labels * capacity
    share = model_width // sections
    stream_shape = shape((tok_dev, model_width), BF16)
    table_shapes = (
        shape((blocks, slots, tok_dev), BF16),
        shape((blocks, tok_dev, slots), BF16),
        shape((blocks, tok_dev, 128), F32),
        shape(ln_gain.shape, F32),
    )
    odd = section_index % 2
    own_block = odd

    def tables(ids, gain, *tokens):
        outputs = table_shapes + (stream_shape,) * (2 * len(tokens))
        return pl.pallas_call(
            functools.partial(tables_kernel, blocks),
            out_shape=outputs,
            in_specs=[pl.BlockSpec(memory_space=pltpu.HBM)] * (2 + len(tokens)),
            out_specs=[VMEM_SPEC] * len(outputs),
            scratch_shapes=[
                pltpu.VMEM((blocks, tok_dev), jnp.int32),
                pltpu.SemaphoreType.DMA((4,)),
            ],
            compiler_params=pltpu.CompilerParams(vmem_limit_bytes=LIMIT),
        )(*map(in_hbm, (ids, gain) + tokens))

    def pick(block):
        return jnp.full((8, 128), block, jnp.int32)

    def exchange(rows, axis):
        return lax.all_to_all(rows, axis, split_axis=0, concat_axis=0, tiled=True)

    ids = routes.reshape(blocks, tok_dev)
    router_rows = router[0].T
    weights = (dense_in[0], dense_out[0], expert_in[0], expert_out[0])
    *own_tables, first, second = tables(ids, ln_gain, tokens_in)
    own = (tuple(own_tables), router_rows, weights)

    def swapped():
        swap = [(source, source + 1 - 2 * (source % 2)) for source in range(sections)]
        arrays = weights + (router_rows, ids, ln_gain)
        *others, other_router, other_ids, other_gain = [
            lax.ppermute(value, "section", swap) for value in arrays
        ]
        return tuple(tables(other_ids, other_gain)), other_router, tuple(others)

    def nothing():
        outputs = table_shapes + (router_rows,) + weights
        found = pl.pallas_call(
            untouched_kernel,
            out_shape=tuple(shape(value.shape, value.dtype) for value in outputs),
            out_specs=[pl.BlockSpec(memory_space=pl.ANY)] * len(outputs),
        )()
        return tuple(found[:4]), found[4], tuple(found[5:])

    other = lax.cond(section_index >= 2, swapped, nothing)
    passed = pl.pallas_call(
        copy_over_kernel,
        out_shape=tuple(shape(value.shape, value.dtype) for value in other[2]),
        in_specs=[pl.BlockSpec(memory_space=pl.ANY)] * 4,
        out_specs=[pl.BlockSpec(memory_space=pl.ANY)] * 4,
        scratch_shapes=[pltpu.SemaphoreType.DMA((4,))],
    )(*other[2])
    other = (other[0], other[1], tuple(passed))

    def layer(block, received, context):
        (send, take, picked, gain), router_part, layer_weights = context
        chosen = pick(block)
        normed, outgoing = kernel_call(
            enter_kernel,
            4,
            (stream_shape, shape((slots, model_width), BF16)),
            pl.CostEstimate(flops=20_000_000_000, transcendentals=0, bytes_accessed=40 << 20),
        )(chosen, received, gain, send)
        incoming = exchange(outgoing.reshape(members, slots // members, model_width), "expert")
        results, base, gate = kernel_call(
            layer_kernel,
            10,
            (
                shape(incoming.shape, BF16),
                shape((tok_dev, model_width), F32),
                shape((tok_dev, 128), F32),
            ),
            pl.CostEstimate(
                flops=12 * tok_dev * model_width * hidden_width,
                transcendentals=3 * tok_dev * hidden_width,
                bytes_accessed=26 << 20,
            ),
        )(chosen, received, normed, incoming, picked, router_part, *layer_weights)
        returned = exchange(results, "expert").reshape(slots, model_width)
        return chosen, base, gate, take, returned

    def run(block, received, context):
        return kernel_call(leave_kernel, 5, stream_shape)(
            *layer(block, received, context)
        )

    def keep(stream):
        return kernel_call(keep_kernel, 1, stream_shape)(stream)

    def late_start(stream):
        return pl.pallas_call(
            functools.partial(wait_kernel, TURNS),
            out_shape=stream_shape,
            in_specs=[VMEM_SPEC],
            out_specs=VMEM_SPEC,
            scratch_shapes=[pltpu.SemaphoreType.DMA((1,))],
        )(stream)

    everyone = [(source, source) for source in range(sections)]
    pair = [(0, 1), (1, 0)] + everyone[2:]
    around = [(source, (source + 1) % sections) for source in range(sections)]
    odd_ring = everyone[0::2] + [(source, (source + 2) % sections) for source in range(1, sections, 2)]
    even_ring = everyone[1::2] + [(source, (source + 2) % sections) for source in range(0, sections, 2)]

    fresh = lax.cond(
        section_index == 0,
        lambda stream: run(0, stream, own),
        lambda stream: jnp.zeros((tok_dev, model_width), BF16),
        first,
    )
    arrived = lax.ppermute(fresh, "section", pair)
    waiting = lax.cond(
        section_index == 0,
        lambda stream: run(1, stream, own),
        lambda stream: jnp.zeros((tok_dev, model_width), BF16),
        second,
    )
    stream = lax.cond(
        section_index == 1,
        lambda arrived, waiting: run(0, late_start(arrived), own),
        lambda arrived, waiting: keep(waiting),
        arrived,
        waiting,
    )
    stream = lax.ppermute(stream, "section", around)

    def chip(number, stream):
        place = section_index - 2 * number
        stream = lax.cond(
            (place == -1) | (place == 0),
            lambda stream: run(own_block, stream, own),
            keep,
            stream,
        )
        stream = lax.cond(
            odd == 1, lambda stream: lax.ppermute(stream, "section", odd_ring), keep, stream
        )
        stream = lax.cond(
            (place == 0) | (place == 1),
            lambda stream: run(own_block, stream, other),
            keep,
            stream,
        )
        return lax.cond(
            odd == 0, lambda stream: lax.ppermute(stream, "section", even_ring), keep, stream
        )

    stream = lax.fori_loop(1, sections // 2, chip, stream)
    pieces_shape = shape((sections, tok_dev, share), BF16)
    pieces = lax.cond(
        section_index == sections - 1,
        lambda stream: kernel_call(finish_kernel, 5, pieces_shape)(*layer(1, stream, own)),
        lambda stream: kernel_call(split_kernel, 1, pieces_shape)(stream),
        stream,
    )
    return kernel_call(gather_kernel, 1, shape((blocks, tok_dev, share), BF16))(
        exchange(pieces, "section")
    )


def solution(mesh):
    placed = (
        P(None, "expert", None),
        P("section", None),
        P("section", None, None),
        P("section", None, None),
        P("section", None, None),
        P("section", "expert", None, None),
        P("section", "expert", None, None),
        P("section", None, "expert", None),
    )
    return jax.shard_map(
        body, mesh=mesh, in_specs=placed, out_specs=P(None, "expert", "section"), check_vma=False
    )
```

profile of v0, /device:TPU:1, one launch (start us, length us, event | category | flops | bytes accessed | tf_op | source)
XLA Modules:
  0.0 1062.6 jit_solution(7811591512248314982)
XLA Ops:
  0.0 1.7 shard_map.82
  1.8 39.4 %collective-permute-start.9 = (bf16[128,1024]{1,0:T(8,128)(2,1)S(1)}, bf16[128,1024]{1,0:T(8,128)(2,1)S(1)}, u32[]{:S(2)}, u32[]{:S(2)}) collective-permute-start(bf16[128,1024]{1,0:T(8,128)(2,1)S(1)} %get-tuple-element.1068), channel_id=1, source_target_pairs={{0,16},{16,0},{32,32},{48,48},{64,64},{80,80},{96,96},{112,112},{1... | collective-permute-start | bytes 786440 | tf_op jit(solution)/shard_map/ppermute | solution.py:326
  41.3 0.2 conditional.9
  41.5 0.9 collective-permute-done.9
  42.4 33.4 %conditional.11 = (bf16[128,1024]{1,0:T(8,128)(2,1)S(1)}) conditional(s32[]{:T(128)} %convert_element_type.46, bf16[128,1024]{1,0:T(8,128)(2,1)S(1)} %get-tuple-element.1067, (bf16[128,1024]{1,0:T(8,128)(2,1)S(1)}, f32[1,1024]{1,0:T(1,128)S(1)}, bf16[2,256,128]{2,1,0:T(8,128)(2,1)S(1)}, f32[2,128,128]{2,1,0:T(8,128)S(1)}, bf16[32,1024]{1,0:T(8,128)(2,1)}, ...), branch_computations={%region_4.5_spmd, %region_5.6_spmd} | conditional | flops 23221225472 | bytes 173281472 | solution.py:333
  42.4 1.1 branch_1_fun.26.received_ref
  43.5 0.0 copy-start
  43.5 0.9 copy-done
  44.5 0.0 copy-start.28
  44.5 0.5 branch_1_fun.27
  45.0 12.4 %all_to_all.57.incoming_ref = bf16[16,16,1024]{2,1,0:T(8,128)(2,1)S(1)} all-to-all(bf16[16,16,1024]{2,1,0:T(8,128)(2,1)S(1)} %bitcast.30), channel_id=1, replica_groups=mesh['section'=8,'expert'=16] {'expert'}, dimensions={0} | all-to-all | bytes 1048576 | tf_op jit(solution)/shard_map/cond/branch_1_fun/all_to_all | solution.py:235
  57.4 0.0 copy-done.3
  57.4 0.0 copy-done.13
  57.4 3.9 branch_1_fun.28
  61.3 13.3 %all_to_all.58 = bf16[16,16,1024]{2,1,0:T(8,128)(2,1)S(1)} all-to-all(bf16[16,16,1024]{2,1,0:T(8,128)(2,1)S(1)} %get-tuple-element.648), channel_id=1, replica_groups=mesh['section'=8,'expert'=16] {'expert'}, dimensions={0} | all-to-all | bytes 1048576 | tf_op jit(solution)/shard_map/cond/branch_1_fun/all_to_all | solution.py:235
  74.6 1.1 branch_1_fun.29
  75.8 0.0 collective-permute-start.10
  75.8 0.0 copy-start.25
  75.8 0.0 copy-start.31
  75.8 0.0 copy-start.32
  75.8 0.1 shard_map.83
  75.9 3.2 collective-permute-done.10
  79.1 0.0 copy-done.31
  79.1 827.4 %while.20 = (s32[]{:T(128)}, bf16[128,1024]{1,0:T(8,128)(2,1)}, pred[]{:T(512)}, s32[]{:T(128)}, pred[]{:T(512)}, /*index=5*/s32[]{:T(128)}, f32[1,1024]{1,0:T(1...) while((s32[]{:T(128)}, bf16[128,1024]{1,0:T(8,128)(2,1)}, ...), condition=%wide.region_17.18_spmd, body=%wide.region_8.17_spmd.sunk | while | flops 46442450944 | bytes 346039136 | solution.py:363
  79.1 31.5 %conditional.18 = (bf16[128,1024]{1,0:T(8,128)(2,1)S(1)}) conditional(s32[]{:T(128)} %convert_element_type.56, bf16[128,1024]{1,0:T(8,128)(2,1)} %get-tuple-element.1012, (s32[]{:T(128)}, bf16[128,1024]{1,0:T(8,128)(2,1)}, f32[1,1024]{1,0:T(1,128)S(1)}, bf16[2,256,128]{2,1,0:T(8,128)(2,1)S(1)}, f32[2,128,128]{2,1,0:T(8,128)S(1)}, ...), branch_computations={%region_9.9_spmd, %region_10.10_spmd} | conditional | flops 23221225472 | bytes 171970688 | solution.py:344
  79.1 0.0 copy-start.4
  79.1 0.0 copy-start.9
  79.2 0.0 copy-start.14
  79.2 0.0 copy-start.19
  79.2 1.6 branch_1_fun.31
  80.8 12.1 %all_to_all.59.incoming_ref = bf16[16,16,1024]{2,1,0:T(8,128)(2,1)S(1)} all-to-all(bf16[16,16,1024]{2,1,0:T(8,128)(2,1)S(1)} %bitcast.22), channel_id=1, replica_groups=mesh['section'=8,'expert'=16] {'expert'}, dimensions={0} | all-to-all | bytes 1048576 | tf_op jit(solution)/shard_map/while/body/eval_jaxpr/cond/branch_1_fun/all_to_all | solution.py:235
  92.9 0.0 copy-done.9
  93.0 4.9 branch_1_fun.32
  97.8 11.7 %all_to_all.60 = bf16[16,16,1024]{2,1,0:T(8,128)(2,1)S(1)} all-to-all(bf16[16,16,1024]{2,1,0:T(8,128)(2,1)S(1)} %get-tuple-element.675), channel_id=1, replica_groups=mesh['section'=8,'expert'=16] {'expert'}, dimensions={0} | all-to-all | bytes 1048576 | tf_op jit(solution)/shard_map/while/body/eval_jaxpr/cond/branch_1_fun/all_to_all | solution.py:235
  109.5 1.1 branch_1_fun.33
  110.6 737.8 %conditional.19 = (bf16[128,1024]{1,0:T(8,128)(2,1)}) conditional(s32[]{:T(128)} %convert_element_type.55, bf16[128,1024]{1,0:T(8,128)(2,1)S(1)} %get-tuple-element.1072, bf16[128,1024]{1,0:T(8,128)(2,1)S(1)} %get-tuple-element.1072), branch_computations={%region_11.11_spmd, %region_12.12_spmd} | conditional | bytes 1048624 | solution.py:350
  110.7 704.7 %collective-permute-start.7 = (bf16[128,1024]{1,0:T(8,128)(2,1)S(1)}, bf16[128,1024]{1,0:T(8,128)(2,1)}, u32[]{:S(2)}, u32[]{:S(2)}) collective-permute-start(bf16[128,1024]{1,0:T(8,128)(2,1)S(1)} %param.11), channel_id=1, source_target_pairs={{0,0},{32,32},{64,64},{96,96},{16,48},{48,80},{80,112},{112,16},{1... | collective-permute-start | bytes 786440 | tf_op jit(solution)/shard_map/while/body/eval_jaxpr/cond/branch_1_fun/ppermute | solution.py:351
  815.4 33.1 %collective-permute-done.7 = bf16[128,1024]{1,0:T(8,128)(2,1)} collective-permute-done((bf16[128,1024]{1,0:T(8,128)(2,1)S(1)}, bf16[128,1024]{1,0:T(8,128)(2,1)}, u32[]{:S(2)}, u32[]{:S(2)}) %collective-permute-start.7) | collective-permute-done | bytes 262176 | tf_op jit(solution)/shard_map/while/body/eval_jaxpr/cond/branch_1_fun/ppermute | solution.py:351
  848.5 1.0 conditional.20
  848.5 1.0 branch_0_fun.11
  849.5 0.7 conditional.21
  849.5 0.7 branch_0_fun.12
  850.2 1.0 conditional.18
  850.2 1.0 branch_0_fun.9
  851.2 42.4 %conditional.19 = (bf16[128,1024]{1,0:T(8,128)(2,1)}) conditional(s32[]{:T(128)} %convert_element_type.55, bf16[128,1024]{1,0:T(8,128)(2,1)S(1)} %get-tuple-element.1072, bf16[128,1024]{1,0:T(8,128)(2,1)S(1)} %get-tuple-element.1072), branch_computations={%region_11.11_spmd, %region_12.12_spmd} | conditional | bytes 1048624 | solution.py:350
  851.2 39.1 %collective-permute-start.7 = (bf16[128,1024]{1,0:T(8,128)(2,1)S(1)}, bf16[128,1024]{1,0:T(8,128)(2,1)}, u32[]{:S(2)}, u32[]{:S(2)}) collective-permute-start(bf16[128,1024]{1,0:T(8,128)(2,1)S(1)} %param.11), channel_id=1, source_target_pairs={{0,0},{32,32},{64,64},{96,96},{16,48},{48,80},{80,112},{112,16},{1... | collective-permute-start | bytes 786440 | tf_op jit(solution)/shard_map/while/body/eval_jaxpr/cond/branch_1_fun/ppermute | solution.py:351
  890.3 3.3 collective-permute-done.7
  893.6 1.0 conditional.20
  893.6 1.0 branch_0_fun.11
  894.5 0.7 conditional.21
  894.6 0.7 branch_0_fun.12
  895.3 1.0 conditional.18
  895.3 1.0 branch_0_fun.9
  896.3 8.5 conditional.19
  896.3 3.9 collective-permute-start.7
  900.2 4.5 collective-permute-done.7
  904.8 1.0 conditional.20
  904.8 1.0 branch_0_fun.11
  905.7 0.7 conditional.21
  905.7 0.7 branch_0_fun.12
  906.5 1.0 conditional.13
  906.5 1.0 branch_0_fun.13
  907.5 154.5 %all_to_all.65.pieces_ref = bf16[8,128,128]{2,1,0:T(8,128)(2,1)S(1)} all-to-all(bf16[8,128,128]{2,1,0:T(8,128)(2,1)S(1)} %get-tuple-element.1071), channel_id=1, replica_groups=mesh['section'=8,'expert'=16] {'section'}, dimensions={0} | all-to-all | bytes 524288 | tf_op jit(solution)/shard_map/all_to_all | solution.py:235
  1062.0 0.6 shard_map.84
  (19 shorter events, 0.1 us)
Async XLA Ops:
  1.8 40.6 %collective-permute-start.9 = (bf16[128,1024]{1,0:T(8,128)(2,1)S(1)}, bf16[128,1024]{1,0:T(8,128)(2,1)S(1)}, u32[]{:S(2)}, u32[]{:S(2)}) collective-permute-start(bf16[128,1024]{1,0:T(8,128)(2,1)S(1)} %get-tuple-element.1068), channel_id=1, source_target_pairs={{0,16},{16,0},{32,32},{48,48},{64,64},{80,80},{96,96},{112,112},{1... | collective-permute-start | bytes 786440 | tf_op jit(solution)/shard_map/ppermute | solution.py:326
  43.5 1.0 copy-start
  44.5 12.9 %copy-start.3 = (bf16[2,1024,2048]{2,1,0:T(8,128)(2,1)S(1)}, bf16[2,1024,2048]{2,1,0:T(8,128)(2,1)}, u32[]{:S(2)}) copy-start(bf16[2,1024,2048]{2,1,0:T(8,128)(2,1)} %get-tuple-element.643.expert_in_ref) | copy-start | bytes 25165828 | tf_op jit(solution)/shard_map/cond
  44.5 12.9 %copy-start.8 = (bf16[2,2048,1024]{2,1,0:T(8,128)(2,1)S(1)}, bf16[2,2048,1024]{2,1,0:T(8,128)(2,1)}, u32[]{:S(2)}) copy-start(bf16[2,2048,1024]{2,1,0:T(8,128)(2,1)} %get-tuple-element.644.expert_out_ref) | copy-start | bytes 25165828 | tf_op jit(solution)/shard_map/cond
  44.5 12.9 %copy-start.13 = (bf16[1024,2048]{1,0:T(8,128)(2,1)S(1)}, bf16[1024,2048]{1,0:T(8,128)(2,1)}, u32[]{:S(2)}) copy-start(bf16[1024,2048]{1,0:T(8,128)(2,1)} %get-tuple-element.641.dense_in_ref) | copy-start | bytes 12582916 | tf_op jit(solution)/shard_map/cond
  44.5 13.0 %copy-start.18 = (bf16[2048,1024]{1,0:T(8,128)(2,1)S(1)}, bf16[2048,1024]{1,0:T(8,128)(2,1)}, u32[]{:S(2)}) copy-start(bf16[2048,1024]{1,0:T(8,128)(2,1)} %get-tuple-element.642.dense_out_ref) | copy-start | bytes 12582916 | tf_op jit(solution)/shard_map/cond
  44.5 13.0 %copy-start.28 = (bf16[32,1024]{1,0:T(8,128)(2,1)S(1)}, bf16[32,1024]{1,0:T(8,128)(2,1)}, u32[]{:S(2)}) copy-start(bf16[32,1024]{1,0:T(8,128)(2,1)} %get-tuple-element.640.router_ref) | copy-start | bytes 196612 | tf_op jit(solution)/shard_map/cond
  75.8 3.3 collective-permute-start.10
  75.8 3.3 copy-start.25
  75.8 3.3 copy-start.31
  75.8 3.3 copy-start.32
  79.1 13.8 %copy-start.4 = (bf16[2,1024,2048]{2,1,0:T(8,128)(2,1)S(1)}, bf16[2,1024,2048]{2,1,0:T(8,128)(2,1)}, u32[]{:S(2)}) copy-start(bf16[2,1024,2048]{2,1,0:T(8,128)(2,1)} %get-tuple-element.670.expert_in_ref) | copy-start | bytes 25165828 | tf_op jit(solution)/shard_map/while/body/eval_jaxpr/cond
  79.1 13.8 %copy-start.9 = (bf16[2,2048,1024]{2,1,0:T(8,128)(2,1)S(1)}, bf16[2,2048,1024]{2,1,0:T(8,128)(2,1)}, u32[]{:S(2)}) copy-start(bf16[2,2048,1024]{2,1,0:T(8,128)(2,1)} %get-tuple-element.671.expert_out_ref) | copy-start | bytes 25165828 | tf_op jit(solution)/shard_map/while/body/eval_jaxpr/cond
  79.2 13.8 %copy-start.14 = (bf16[1024,2048]{1,0:T(8,128)(2,1)S(1)}, bf16[1024,2048]{1,0:T(8,128)(2,1)}, u32[]{:S(2)}) copy-start(bf16[1024,2048]{1,0:T(8,128)(2,1)} %get-tuple-element.668.dense_in_ref) | copy-start | bytes 12582916 | tf_op jit(solution)/shard_map/while/body/eval_jaxpr/cond
  79.2 13.8 %copy-start.19 = (bf16[2048,1024]{1,0:T(8,128)(2,1)S(1)}, bf16[2048,1024]{1,0:T(8,128)(2,1)}, u32[]{:S(2)}) copy-start(bf16[2048,1024]{1,0:T(8,128)(2,1)} %get-tuple-element.669.dense_out_ref) | copy-start | bytes 12582916 | tf_op jit(solution)/shard_map/while/body/eval_jaxpr/cond
  110.7 737.8 %collective-permute-start.7 = (bf16[128,1024]{1,0:T(8,128)(2,1)S(1)}, bf16[128,1024]{1,0:T(8,128)(2,1)}, u32[]{:S(2)}, u32[]{:S(2)}) collective-permute-start(bf16[128,1024]{1,0:T(8,128)(2,1)S(1)} %param.11), channel_id=1, source_target_pairs={{0,0},{32,32},{64,64},{96,96},{16,48},{48,80},{80,112},{112,16},{1... | collective-permute-start | bytes 786440 | tf_op jit(solution)/shard_map/while/body/eval_jaxpr/cond/branch_1_fun/ppermute | solution.py:351
  851.2 42.4 %collective-permute-start.7 = (bf16[128,1024]{1,0:T(8,128)(2,1)S(1)}, bf16[128,1024]{1,0:T(8,128)(2,1)}, u32[]{:S(2)}, u32[]{:S(2)}) collective-permute-start(bf16[128,1024]{1,0:T(8,128)(2,1)S(1)} %param.11), channel_id=1, source_target_pairs={{0,0},{32,32},{64,64},{96,96},{16,48},{48,80},{80,112},{112,16},{1... | collective-permute-start | bytes 786440 | tf_op jit(solution)/shard_map/while/body/eval_jaxpr/cond/branch_1_fun/ppermute | solution.py:351
  896.3 8.5 collective-permute-start.7
where the time goes:
time: 1060 us
  starting transfers between devices  787 us (74%)
  blocking collectives  204 us (19%)
  waiting for transfers between devices  45 us (4%)
  Pallas kernels  24.7 us (2%)
    ppermute x3, starting transfers between devices, chip(): lax.ppermute(stream, 'section', odd_ring)  748 us
    all_to_all x5, blocking collectives, exchange(): return lax.all_to_all(rows, axis, split_axis=0, concat_axis=0, tiled=True)  204 us
    ppermute x3, waiting for transfers between devices, chip(): lax.ppermute(stream, 'section', odd_ring)  40.9 us
    ppermute x1, starting transfers between devices, body(): arrived = lax.ppermute(fresh, 'section', pair)  39.4 us
  transfers between devices with their start and end apart: 5, of which 5 were waited for; matrix products, arithmetic and copies ran while one was open for 0% of the time, Pallas kernels for 0%

commit v1 on v0

--- a/solution.py
+++ b/solution.py
@@ -22,7 +22,7 @@
     return lax.dot_general(a, b, (((1,), (1,)), ((), ())), preferred_element_type=F32)
 
 
-def tables_kernel(blocks, routes_ref, gain_ref, *refs):
+def make_tables(blocks, routes_ref, gain_ref, *refs):
     tokens_ref = refs[0] if len(refs) == 9 else None
     send_ref, take_ref, picked_ref, held_gain_ref = refs[1:5] if tokens_ref is not None else refs[:4]
     ids_ref, sems = refs[-2:]
@@ -58,6 +58,13 @@
         copy.wait()
 
 
+def tables_kernel(blocks, always, *refs):
+    if always:
+        make_tables(blocks, *refs)
+    else:
+        pl.when(lax.axis_index("section") >= 2)(functools.partial(make_tables, blocks, *refs))
+
+
 def of_block(pick_ref, table_ref):
     rows, lanes = table_ref.shape[1:]
     second = jnp.broadcast_to(pick_ref[:1, :1] == 1, (rows, lanes))
@@ -156,18 +163,27 @@
 
 
 def copy_over_kernel(*refs):
-    count = len(refs) // 2
-    sems = refs[-1]
+    count = (len(refs) - 1) // 3
+    sources, targets, stages, sems = refs[: count + 1], refs[count + 1 : 2 * count + 2], refs[2 * count + 2 : -1], refs[-1]
 
     @pl.when(lax.axis_index("section") >= 2)
     def _():
-        copies = [
-            pltpu.make_async_copy(refs[n], refs[count + n], sems.at[n]) for n in range(count)
+        reads = [
+            pltpu.make_async_copy(source, stage, sems.at[0, n])
+            for n, (source, stage) in enumerate(zip(sources, stages + targets[-1:]))
         ]
-        for copy in copies:
-            copy.start()
-        for copy in copies:
-            copy.wait()
+        writes = [
+            pltpu.make_async_copy(stage, target, sems.at[1, n])
+            for n, (stage, target) in enumerate(zip(stages, targets))
+        ]
+        for read in reads:
+            read.start()
+        for read, write in zip(reads, writes):
+            read.wait()
+            write.start()
+        reads[-1].wait()
+        for write in writes:
+            write.wait()
 
 
 def in_hbm(value):
@@ -214,10 +230,10 @@
     odd = section_index % 2
     own_block = odd
 
-    def tables(ids, gain, *tokens):
+    def tables(always, ids, gain, *tokens):
         outputs = table_shapes + (stream_shape,) * (2 * len(tokens))
         return pl.pallas_call(
-            functools.partial(tables_kernel, blocks),
+            functools.partial(tables_kernel, blocks, always),
             out_shape=outputs,
             in_specs=[pl.BlockSpec(memory_space=pltpu.HBM)] * (2 + len(tokens)),
             out_specs=[VMEM_SPEC] * len(outputs),
@@ -237,35 +253,35 @@
     ids = routes.reshape(blocks, tok_dev)
     router_rows = router[0].T
     weights = (dense_in[0], dense_out[0], expert_in[0], expert_out[0])
-    *own_tables, first, second = tables(ids, ln_gain, tokens_in)
+    *own_tables, first, second = tables(True, ids, ln_gain, tokens_in)
     own = (tuple(own_tables), router_rows, weights)
 
     def swapped():
         swap = [(source, source + 1 - 2 * (source % 2)) for source in range(sections)]
         arrays = weights + (router_rows, ids, ln_gain)
-        *others, other_router, other_ids, other_gain = [
-            lax.ppermute(value, "section", swap) for value in arrays
-        ]
-        return tuple(tables(other_ids, other_gain)), other_router, tuple(others)
+        return tuple(lax.ppermute(value, "section", swap) for value in arrays)
 
     def nothing():
-        outputs = table_shapes + (router_rows,) + weights
-        found = pl.pallas_call(
-            untouched_kernel,
-            out_shape=tuple(shape(value.shape, value.dtype) for value in outputs),
-            out_specs=[pl.BlockSpec(memory_space=pl.ANY)] * len(outputs),
-        )()
-        return tuple(found[:4]), found[4], tuple(found[5:])
-
-    other = lax.cond(section_index >= 2, swapped, nothing)
-    passed = pl.pallas_call(
+        arrays = weights + (router_rows, ids, ln_gain)
+        return tuple(
+            pl.pallas_call(
+                untouched_kernel,
+                out_shape=tuple(shape(value.shape, value.dtype) for value in arrays),
+                out_specs=[pl.BlockSpec(memory_space=pl.ANY)] * len(arrays),
+            )()
+        )
+
+    *others, other_ids, other_gain = lax.cond(section_index >= 2, swapped, nothing)
+    *other_weights, other_router = pl.pallas_call(
         copy_over_kernel,
-        out_shape=tuple(shape(value.shape, value.dtype) for value in other[2]),
-        in_specs=[pl.BlockSpec(memory_space=pl.ANY)] * 4,
-        out_specs=[pl.BlockSpec(memory_space=pl.ANY)] * 4,
-        scratch_shapes=[pltpu.SemaphoreType.DMA((4,))],
-    )(*other[2])
-    other = (other[0], other[1], tuple(passed))
+        out_shape=tuple(shape(value.shape, value.dtype) for value in others),
+        in_specs=[pl.BlockSpec(memory_space=pl.ANY)] * 5,
+        out_specs=[pl.BlockSpec(memory_space=pl.ANY)] * 4 + [VMEM_SPEC],
+        scratch_shapes=[pltpu.VMEM(value.shape, BF16) for value in weights]
+        + [pltpu.SemaphoreType.DMA((2, 5))],
+        compiler_params=pltpu.CompilerParams(vmem_limit_bytes=LIMIT),
+    )(*others)
+    other = (tuple(tables(False, other_ids, other_gain)), other_router, tuple(other_weights))
 
     def layer(block, received, context):
         (send, take, picked, gain), router_part, layer_weights = context
@@ -348,7 +364,7 @@
             stream,
         )
         stream = lax.cond(
-            odd == 1, lambda stream: lax.ppermute(stream, "section", odd_ring), keep, stream
+            odd == 1, lambda stream: keep(lax.ppermute(stream, "section", odd_ring)), keep, stream
         )
         stream = lax.cond(
             (place == 0) | (place == 1),
@@ -357,7 +373,7 @@
             stream,
         )
         return lax.cond(
-            odd == 0, lambda stream: lax.ppermute(stream, "section", even_ring), keep, stream
+            odd == 0, lambda stream: keep(lax.ppermute(stream, "section", even_ring)), keep, stream
         )
 
     stream = lax.fori_loop(1, sections // 2, chip, stream)

time: 1060 us -> 328 us (0.31)
  starting transfers between devices: 787 us -> 109 us
  blocking collectives: 204 us -> 176 us
  waiting for transfers between devices: 45 us -> 18.4 us
    ppermute x3, starting transfers between devices: 748 us -> 69.3 us  [chip(): lax.ppermute(stream, 'section', odd_ring)]
    all_to_all x5, blocking collectives: 204 us -> 176 us  [exchange(): return lax.all_to_all(rows, axis, split_axis=0, concat_axis=0, tiled=True)]
    ppermute x3, waiting for transfers between devices: 40.9 us -> 14.2 us  [chip(): lax.ppermute(stream, 'section', odd_ring)]
where the time goes in v1:
time: 328 us
  blocking collectives  176 us (54%)
  starting transfers between devices  109 us (33%)
  Pallas kernels  22 us (7%)
  waiting for transfers between devices  18.4 us (6%)
    all_to_all x5, blocking collectives, exchange(): return lax.all_to_all(rows, axis, split_axis=0, concat_axis=0, tiled=True)  176 us
    ppermute x3, starting transfers between devices, chip(): lax.ppermute(stream, 'section', odd_ring)  69.3 us
    ppermute x1, starting transfers between devices, body(): arrived = lax.ppermute(fresh, 'section', pair)  39.4 us
    ppermute x3, waiting for transfers between devices, chip(): lax.ppermute(stream, 'section', odd_ring)  14.2 us
    pallas_call x2, Pallas kernels, layer(): kernel_call(layer_kernel, 10, (shape(incoming.shape, BF16), shape((tok_de...  8.79 us
  transfers between devices with their start and end apart: 5, of which 5 were waited for; matrix products, arithmetic and copies ran while one was open for 0% of the time, Pallas kernels for 0%

profile of v1, /device:TPU:1, one launch (start us, length us, event | category | flops | bytes accessed | tf_op | source)
XLA Modules:
  0.0 327.6 jit_solution(9047778947013562384)
XLA Ops:
  0.0 1.7 shard_map.82
  1.8 39.4 %collective-permute-start.9 = (bf16[128,1024]{1,0:T(8,128)(2,1)S(1)}, bf16[128,1024]{1,0:T(8,128)(2,1)S(1)}, u32[]{:S(2)}, u32[]{:S(2)}) collective-permute-start(bf16[128,1024]{1,0:T(8,128)(2,1)S(1)} %get-tuple-element.1066), channel_id=1, source_target_pairs={{0,16},{16,0},{32,32},{48,48},{64,64},{80,80},{96,96},{112,112},{1... | collective-permute-start | bytes 786440 | tf_op jit(solution)/shard_map/ppermute | solution.py:342
  41.3 1.1 collective-permute-done.9
  42.4 33.6 %conditional.11 = (bf16[128,1024]{1,0:T(8,128)(2,1)S(1)}) conditional(s32[]{:T(128)} %convert_element_type.46, bf16[128,1024]{1,0:T(8,128)(2,1)S(1)} %get-tuple-element.1065, (bf16[128,1024]{1,0:T(8,128)(2,1)S(1)}, f32[1,1024]{1,0:T(1,128)S(1)}, bf16[2,256,128]{2,1,0:T(8,128)(2,1)S(1)}, f32[2,128,128]{2,1,0:T(8,128)S(1)}, bf16[32,1024]{1,0:T(8,128)(2,1)}, ...), branch_computations={%region_4.5_spmd, %region_5.6_spmd} | conditional | flops 23221225472 | bytes 173281472 | solution.py:349
  42.4 1.1 branch_1_fun.27.received_ref
  43.5 0.0 copy-start
  43.5 0.9 copy-done
  44.4 0.0 copy-start.3
  44.4 0.0 copy-start.8
  44.4 0.0 copy-start.13
  44.4 0.0 copy-start.18
  44.4 0.0 copy-start.28
  44.5 0.5 branch_1_fun.28
  45.0 12.4 %all_to_all.57.incoming_ref = bf16[16,16,1024]{2,1,0:T(8,128)(2,1)S(1)} all-to-all(bf16[16,16,1024]{2,1,0:T(8,128)(2,1)S(1)} %bitcast.30), channel_id=1, replica_groups=mesh['section'=8,'expert'=16] {'expert'}, dimensions={0} | all-to-all | bytes 1048576 | tf_op jit(solution)/shard_map/cond/branch_1_fun/all_to_all | solution.py:251
  57.4 0.0 copy-done.3
  57.4 0.0 copy-done.8
  57.4 0.0 copy-done.13
  57.4 0.0 copy-done.18
  57.4 0.0 copy-done.28
  57.4 3.9 %branch_1_fun.29 = (bf16[16,16,1024]{2,1,0:T(8,128)(2,1)S(1)}, f32[128,1024]{1,0:T(8,128)S(1)}, f32[128,128]{1,0:T(8,128)S(1)}) custom-call(s32[8,128]{1,0:T(8,128)S(1)} %broadcast_9_pick_ref.0.pick_ref, bf16[128,1024]{1,0:T(8,128)(2,1)S(1)} %copy-done, bf16[128,1024]{1,0:T(8,128)(2,1)S(1)} %get-tuple-element.637.normed_ref, ...), custom_call_target="tpu_custom_call" | custom-call | flops 3221225472 | bytes 27262976 | tf_op jit(solution)/shard_map/cond/branch_1_fun/pallas_call | solution.py:296
  61.4 13.3 %all_to_all.58 = bf16[16,16,1024]{2,1,0:T(8,128)(2,1)S(1)} all-to-all(bf16[16,16,1024]{2,1,0:T(8,128)(2,1)S(1)} %get-tuple-element.648), channel_id=1, replica_groups=mesh['section'=8,'expert'=16] {'expert'}, dimensions={0} | all-to-all | bytes 1048576 | tf_op jit(solution)/shard_map/cond/branch_1_fun/all_to_all | solution.py:251
  74.7 1.1 branch_1_fun.30
  76.0 0.0 collective-permute-start.10
  76.1 0.1 shard_map.83
  76.1 0.0 copy-start.25
  76.1 0.1 shard_map.84
  76.3 3.1 collective-permute-done.10
  79.4 0.0 copy-done.25
  79.4 119.5 %while.20 = (s32[]{:T(128)}, bf16[128,1024]{1,0:T(8,128)(2,1)}, pred[]{:T(512)}, s32[]{:T(128)}, pred[]{:T(512)}, /*index=5*/s32[]{:T(128)}, f32[1,1024]{1,0:T(1...) while((s32[]{:T(128)}, bf16[128,1024]{1,0:T(8,128)(2,1)}, ...), condition=%wide.region_17.18_spmd, body=%wide.region_8.17_spmd.sunk | while | flops 46442450944 | bytes 346039136 | solution.py:379
  79.4 31.5 %conditional.18 = (bf16[128,1024]{1,0:T(8,128)(2,1)S(1)}) conditional(s32[]{:T(128)} %convert_element_type.56, bf16[128,1024]{1,0:T(8,128)(2,1)} %get-tuple-element.1010, (s32[]{:T(128)}, bf16[128,1024]{1,0:T(8,128)(2,1)}, f32[1,1024]{1,0:T(1,128)S(1)}, bf16[2,256,128]{2,1,0:T(8,128)(2,1)S(1)}, f32[2,128,128]{2,1,0:T(8,128)S(1)}, ...), branch_computations={%region_9.9_spmd, %region_10.10_spmd} | conditional | flops 23221225472 | bytes 171970688 | solution.py:360
  79.4 0.0 copy-start.14
  79.4 0.0 copy-start.19
  79.4 1.6 branch_1_fun.31
  81.0 12.1 %all_to_all.59.incoming_ref = bf16[16,16,1024]{2,1,0:T(8,128)(2,1)S(1)} all-to-all(bf16[16,16,1024]{2,1,0:T(8,128)(2,1)S(1)} %bitcast.22), channel_id=1, replica_groups=mesh['section'=8,'expert'=16] {'expert'}, dimensions={0} | all-to-all | bytes 1048576 | tf_op jit(solution)/shard_map/while/body/eval_jaxpr/cond/branch_1_fun/all_to_all | solution.py:251
  93.2 0.0 copy-done.4
  93.2 0.0 copy-done.9
  93.2 0.0 copy-done.14
  93.2 0.0 copy-done.19
  93.2 4.9 %branch_1_fun.32 = (bf16[16,16,1024]{2,1,0:T(8,128)(2,1)S(1)}, f32[128,1024]{1,0:T(8,128)S(1)}, f32[128,128]{1,0:T(8,128)S(1)}) custom-call(s32[8,128]{1,0:T(8,128)S(1)} %broadcast_in_dim.4.pick_ref, bf16[128,1024]{1,0:T(8,128)(2,1)} %get-tuple-element.657.received_ref, bf16[128,1024]{1,0:T(8,128)(2,1)S(1)} %get-tuple-element.660.normed_ref, ...), custom_call_target="tpu_custom_call" | custom-call | flops 3221225472 | bytes 27262976 | tf_op jit(solution)/shard_map/while/body/eval_jaxpr/cond/branch_1_fun/pallas_call | solution.py:296
  98.1 11.7 %all_to_all.60 = bf16[16,16,1024]{2,1,0:T(8,128)(2,1)S(1)} all-to-all(bf16[16,16,1024]{2,1,0:T(8,128)(2,1)S(1)} %get-tuple-element.671), channel_id=1, replica_groups=mesh['section'=8,'expert'=16] {'expert'}, dimensions={0} | all-to-all | bytes 1048576 | tf_op jit(solution)/shard_map/while/body/eval_jaxpr/cond/branch_1_fun/all_to_all | solution.py:251
  109.7 1.1 branch_1_fun.33
  110.9 8.4 %conditional.19 = (bf16[128,1024]{1,0:T(8,128)(2,1)S(1)}) conditional(s32[]{:T(128)} %convert_element_type.55, bf16[128,1024]{1,0:T(8,128)(2,1)S(1)} %get-tuple-element.1070, bf16[128,1024]{1,0:T(8,128)(2,1)S(1)} %get-tuple-element.1070), branch_computations={%region_11.11_spmd, %region_12.12_spmd} | conditional | bytes 1048624 | solution.py:366
  110.9 1.9 collective-permute-start.7
  112.8 6.4 %collective-permute-done.7.source_ref = bf16[128,1024]{1,0:T(8,128)(2,1)S(1)} collective-permute-done((bf16[128,1024]{1,0:T(8,128)(2,1)S(1)}, bf16[128,1024]{1,0:T(8,128)(2,1)S(1)}, u32[]{:S(2)}, u32[]{:S(2)}) %collective-permute-start.7) | collective-permute-done | bytes 262176 | tf_op jit(solution)/shard_map/while/body/eval_jaxpr/cond/branch_1_fun/ppermute | solution.py:367
  119.3 0.7 conditional.21
  119.3 0.7 branch_0_fun.12
  120.0 1.0 conditional.18
  120.0 1.0 branch_0_fun.9
  121.0 66.9 %conditional.19 = (bf16[128,1024]{1,0:T(8,128)(2,1)S(1)}) conditional(s32[]{:T(128)} %convert_element_type.55, bf16[128,1024]{1,0:T(8,128)(2,1)S(1)} %get-tuple-element.1070, bf16[128,1024]{1,0:T(8,128)(2,1)S(1)} %get-tuple-element.1070), branch_computations={%region_11.11_spmd, %region_12.12_spmd} | conditional | bytes 1048624 | solution.py:366
  121.0 63.6 %collective-permute-start.7 = (bf16[128,1024]{1,0:T(8,128)(2,1)S(1)}, bf16[128,1024]{1,0:T(8,128)(2,1)S(1)}, u32[]{:S(2)}, u32[]{:S(2)}) collective-permute-start(bf16[128,1024]{1,0:T(8,128)(2,1)S(1)} %param.11), channel_id=1, source_target_pairs={{0,0},{32,32},{64,64},{96,96},{16,48},{48,80},{80,112},{112,16},{1... | collective-permute-start | bytes 786440 | tf_op jit(solution)/shard_map/while/body/eval_jaxpr/cond/branch_1_fun/ppermute | solution.py:367
  184.6 3.3 %collective-permute-done.7.source_ref = bf16[128,1024]{1,0:T(8,128)(2,1)S(1)} collective-permute-done((bf16[128,1024]{1,0:T(8,128)(2,1)S(1)}, bf16[128,1024]{1,0:T(8,128)(2,1)S(1)}, u32[]{:S(2)}, u32[]{:S(2)}) %collective-permute-start.7) | collective-permute-done | bytes 262176 | tf_op jit(solution)/shard_map/while/body/eval_jaxpr/cond/branch_1_fun/ppermute | solution.py:367
  188.0 0.7 conditional.21
  188.0 0.7 branch_0_fun.12
  188.7 1.0 conditional.18
  188.7 1.0 branch_0_fun.9
  189.7 8.4 %conditional.19 = (bf16[128,1024]{1,0:T(8,128)(2,1)S(1)}) conditional(s32[]{:T(128)} %convert_element_type.55, bf16[128,1024]{1,0:T(8,128)(2,1)S(1)} %get-tuple-element.1070, bf16[128,1024]{1,0:T(8,128)(2,1)S(1)} %get-tuple-element.1070), branch_computations={%region_11.11_spmd, %region_12.12_spmd} | conditional | bytes 1048624 | solution.py:366
  189.7 3.8 %collective-permute-start.7 = (bf16[128,1024]{1,0:T(8,128)(2,1)S(1)}, bf16[128,1024]{1,0:T(8,128)(2,1)S(1)}, u32[]{:S(2)}, u32[]{:S(2)}) collective-permute-start(bf16[128,1024]{1,0:T(8,128)(2,1)S(1)} %param.11), channel_id=1, source_target_pairs={{0,0},{32,32},{64,64},{96,96},{16,48},{48,80},{80,112},{112,16},{1... | collective-permute-start | bytes 786440 | tf_op jit(solution)/shard_map/while/body/eval_jaxpr/cond/branch_1_fun/ppermute | solution.py:367
  193.5 4.5 %collective-permute-done.7.source_ref = bf16[128,1024]{1,0:T(8,128)(2,1)S(1)} collective-permute-done((bf16[128,1024]{1,0:T(8,128)(2,1)S(1)}, bf16[128,1024]{1,0:T(8,128)(2,1)S(1)}, u32[]{:S(2)}, u32[]{:S(2)}) %collective-permute-start.7) | collective-permute-done | bytes 262176 | tf_op jit(solution)/shard_map/while/body/eval_jaxpr/cond/branch_1_fun/ppermute | solution.py:367
  198.1 0.7 conditional.21
  198.1 0.7 branch_0_fun.12
  198.8 1.3 conditional.13
  198.8 1.0 branch_0_fun.13
  200.1 126.8 %all_to_all.65.pieces_ref = bf16[8,128,128]{2,1,0:T(8,128)(2,1)S(1)} all-to-all(bf16[8,128,128]{2,1,0:T(8,128)(2,1)S(1)} %get-tuple-element.1069), channel_id=1, replica_groups=mesh['section'=8,'expert'=16] {'section'}, dimensions={0} | all-to-all | bytes 524288 | tf_op jit(solution)/shard_map/all_to_all | solution.py:251
  326.9 0.6 shard_map.85
  (19 shorter events, 0.4 us)
Async XLA Ops:
  1.8 40.6 %collective-permute-start.9 = (bf16[128,1024]{1,0:T(8,128)(2,1)S(1)}, bf16[128,1024]{1,0:T(8,128)(2,1)S(1)}, u32[]{:S(2)}, u32[]{:S(2)}) collective-permute-start(bf16[128,1024]{1,0:T(8,128)(2,1)S(1)} %get-tuple-element.1066), channel_id=1, source_target_pairs={{0,16},{16,0},{32,32},{48,48},{64,64},{80,80},{96,96},{112,112},{1... | collective-permute-start | bytes 786440 | tf_op jit(solution)/shard_map/ppermute | solution.py:342
  43.5 1.0 copy-start
  44.4 13.0 %copy-start.3 = (bf16[2,1024,2048]{2,1,0:T(8,128)(2,1)S(1)}, bf16[2,1024,2048]{2,1,0:T(8,128)(2,1)}, u32[]{:S(2)}) copy-start(bf16[2,1024,2048]{2,1,0:T(8,128)(2,1)} %get-tuple-element.643.expert_in_ref) | copy-start | bytes 25165828 | tf_op jit(solution)/shard_map/cond
  44.4 13.0 %copy-start.8 = (bf16[2,2048,1024]{2,1,0:T(8,128)(2,1)S(1)}, bf16[2,2048,1024]{2,1,0:T(8,128)(2,1)}, u32[]{:S(2)}) copy-start(bf16[2,2048,1024]{2,1,0:T(8,128)(2,1)} %get-tuple-element.644.expert_out_ref) | copy-start | bytes 25165828 | tf_op jit(solution)/shard_map/cond
  44.4 13.0 %copy-start.13 = (bf16[1024,2048]{1,0:T(8,128)(2,1)S(1)}, bf16[1024,2048]{1,0:T(8,128)(2,1)}, u32[]{:S(2)}) copy-start(bf16[1024,2048]{1,0:T(8,128)(2,1)} %get-tuple-element.641.dense_in_ref) | copy-start | bytes 12582916 | tf_op jit(solution)/shard_map/cond
  44.4 13.0 %copy-start.18 = (bf16[2048,1024]{1,0:T(8,128)(2,1)S(1)}, bf16[2048,1024]{1,0:T(8,128)(2,1)}, u32[]{:S(2)}) copy-start(bf16[2048,1024]{1,0:T(8,128)(2,1)} %get-tuple-element.642.dense_out_ref) | copy-start | bytes 12582916 | tf_op jit(solution)/shard_map/cond
  44.4 13.0 %copy-start.28 = (bf16[32,1024]{1,0:T(8,128)(2,1)S(1)}, bf16[32,1024]{1,0:T(8,128)(2,1)}, u32[]{:S(2)}) copy-start(bf16[32,1024]{1,0:T(8,128)(2,1)} %get-tuple-element.640.router_ref) | copy-start | bytes 196612 | tf_op jit(solution)/shard_map/cond
  76.0 3.3 %collective-permute-start.10 = (bf16[128,1024]{1,0:T(8,128)(2,1)S(1)}, bf16[128,1024]{1,0:T(8,128)(2,1)}, u32[]{:S(2)}, u32[]{:S(2)}) collective-permute-start(bf16[128,1024]{1,0:T(8,128)(2,1)S(1)} %get-tuple-element.1067), channel_id=1, source_target_pairs={{0,16},{16,32},{32,48},{48,64},{64,80},{80,96},{96,112},{112,0},{1... | collective-permute-start | bytes 786440 | tf_op jit(solution)/shard_map/ppermute | solution.py:356
  76.1 3.2 copy-start.25
  79.4 13.8 %copy-start.4 = (bf16[2,1024,2048]{2,1,0:T(8,128)(2,1)S(1)}, bf16[2,1024,2048]{2,1,0:T(8,128)(2,1)}, u32[]{:S(2)}) copy-start(bf16[2,1024,2048]{2,1,0:T(8,128)(2,1)} %get-tuple-element.666.expert_in_ref) | copy-start | bytes 25165828 | tf_op jit(solution)/shard_map/while/body/eval_jaxpr/cond
  79.4 13.8 %copy-start.9 = (bf16[2,2048,1024]{2,1,0:T(8,128)(2,1)S(1)}, bf16[2,2048,1024]{2,1,0:T(8,128)(2,1)}, u32[]{:S(2)}) copy-start(bf16[2,2048,1024]{2,1,0:T(8,128)(2,1)} %get-tuple-element.667.expert_out_ref) | copy-start | bytes 25165828 | tf_op jit(solution)/shard_map/while/body/eval_jaxpr/cond
  79.4 13.8 %copy-start.14 = (bf16[1024,2048]{1,0:T(8,128)(2,1)S(1)}, bf16[1024,2048]{1,0:T(8,128)(2,1)}, u32[]{:S(2)}) copy-start(bf16[1024,2048]{1,0:T(8,128)(2,1)} %get-tuple-element.664.dense_in_ref) | copy-start | bytes 12582916 | tf_op jit(solution)/shard_map/while/body/eval_jaxpr/cond
  79.4 13.8 %copy-start.19 = (bf16[2048,1024]{1,0:T(8,128)(2,1)S(1)}, bf16[2048,1024]{1,0:T(8,128)(2,1)}, u32[]{:S(2)}) copy-start(bf16[2048,1024]{1,0:T(8,128)(2,1)} %get-tuple-element.665.dense_out_ref) | copy-start | bytes 12582916 | tf_op jit(solution)/shard_map/while/body/eval_jaxpr/cond
  110.9 8.3 %collective-permute-start.7 = (bf16[128,1024]{1,0:T(8,128)(2,1)S(1)}, bf16[128,1024]{1,0:T(8,128)(2,1)S(1)}, u32[]{:S(2)}, u32[]{:S(2)}) collective-permute-start(bf16[128,1024]{1,0:T(8,128)(2,1)S(1)} %param.11), channel_id=1, source_target_pairs={{0,0},{32,32},{64,64},{96,96},{16,48},{48,80},{80,112},{112,16},{1... | collective-permute-start | bytes 786440 | tf_op jit(solution)/shard_map/while/body/eval_jaxpr/cond/branch_1_fun/ppermute | solution.py:367
  121.0 66.9 %collective-permute-start.7 = (bf16[128,1024]{1,0:T(8,128)(2,1)S(1)}, bf16[128,1024]{1,0:T(8,128)(2,1)S(1)}, u32[]{:S(2)}, u32[]{:S(2)}) collective-permute-start(bf16[128,1024]{1,0:T(8,128)(2,1)S(1)} %param.11), channel_id=1, source_target_pairs={{0,0},{32,32},{64,64},{96,96},{16,48},{48,80},{80,112},{112,16},{1... | collective-permute-start | bytes 786440 | tf_op jit(solution)/shard_map/while/body/eval_jaxpr/cond/branch_1_fun/ppermute | solution.py:367
  189.7 8.3 %collective-permute-start.7 = (bf16[128,1024]{1,0:T(8,128)(2,1)S(1)}, bf16[128,1024]{1,0:T(8,128)(2,1)S(1)}, u32[]{:S(2)}, u32[]{:S(2)}) collective-permute-start(bf16[128,1024]{1,0:T(8,128)(2,1)S(1)} %param.11), channel_id=1, source_target_pairs={{0,0},{32,32},{64,64},{96,96},{16,48},{48,80},{80,112},{112,16},{1... | collective-permute-start | bytes 786440 | tf_op jit(solution)/shard_map/while/body/eval_jaxpr/cond/branch_1_fun/ppermute | solution.py:367

commit v2 on v1

--- a/solution.py
+++ b/solution.py
@@ -11,7 +11,7 @@
 F32 = jnp.float32
 VMEM_SPEC = pl.BlockSpec(memory_space=pltpu.VMEM)
 LIMIT = 30 << 20
-TURNS = 8
+TURNS = 36
 
 
 def dot(a, b):
@@ -23,13 +23,13 @@
 
 
 def make_tables(blocks, routes_ref, gain_ref, *refs):
-    tokens_ref = refs[0] if len(refs) == 9 else None
-    send_ref, take_ref, picked_ref, held_gain_ref = refs[1:5] if tokens_ref is not None else refs[:4]
+    tokens_ref = refs[0] if len(refs) == 8 else None
+    send_ref, picked_ref, held_gain_ref = refs[1:4] if tokens_ref is not None else refs[:3]
     ids_ref, sems = refs[-2:]
     tokens = ids_ref.shape[1]
     moves = [(routes_ref, ids_ref), (gain_ref, held_gain_ref)]
     if tokens_ref is not None:
-        moves += [(tokens_ref.at[0], refs[5]), (tokens_ref.at[1], refs[6])]
+        moves += [(tokens_ref.at[0], refs[4]), (tokens_ref.at[1], refs[5])]
     copies = [
         pltpu.make_async_copy(source, target, sems.at[number])
         for number, (source, target) in enumerate(moves)
@@ -52,7 +52,6 @@
         slot = ids * capacity + position
         send = (lax.broadcasted_iota(jnp.int32, (slots, tokens), 0) == slot).astype(F32)
         send_ref[block] = send.astype(BF16)
-        take_ref[block] = send.T.astype(BF16)
         picked_ref[block] = picked.T
     for copy in copies[1:]:
         copy.wait()
@@ -117,13 +116,13 @@
         result_ref[:, window, :] = found.reshape(sources, half, model_width)
 
 
-def stream_after(pick_ref, base_ref, gate_ref, take_ref, returned_ref):
-    routed = dot(of_block(pick_ref, take_ref).astype(BF16), returned_ref[...])
+def stream_after(pick_ref, base_ref, gate_ref, send_ref, returned_ref):
+    routed = dot(of_block(pick_ref, send_ref).T.astype(BF16), returned_ref[...])
     return (base_ref[...] + gate_ref[:, :1] * routed).astype(BF16)
 
 
-def leave_kernel(pick_ref, base_ref, gate_ref, take_ref, returned_ref, stream_ref):
-    stream_ref[...] = stream_after(pick_ref, base_ref, gate_ref, take_ref, returned_ref)
+def leave_kernel(pick_ref, base_ref, gate_ref, send_ref, returned_ref, stream_ref):
+    stream_ref[...] = stream_after(pick_ref, base_ref, gate_ref, send_ref, returned_ref)
 
 
 def put_shares(stream, out_ref):
@@ -132,8 +131,8 @@
         out_ref[number] = stream[:, number * share : (number + 1) * share]
 
 
-def finish_kernel(pick_ref, base_ref, gate_ref, take_ref, returned_ref, out_ref):
-    put_shares(stream_after(pick_ref, base_ref, gate_ref, take_ref, returned_ref), out_ref)
+def finish_kernel(pick_ref, base_ref, gate_ref, send_ref, returned_ref, out_ref):
+    put_shares(stream_after(pick_ref, base_ref, gate_ref, send_ref, returned_ref), out_ref)
 
 
 def split_kernel(stream_ref, out_ref):
@@ -141,8 +140,9 @@
 
 
 def gather_kernel(pieces_ref, out_ref):
-    out_ref[0] = pieces_ref[0]
-    out_ref[1] = pieces_ref[pieces_ref.shape[0] - 1]
+    last = pieces_ref.shape[0] - 1
+    out_ref[0] = pieces_ref[last - 1]
+    out_ref[1] = pieces_ref[last]
 
 
 def untouched_kernel(*refs):
@@ -150,10 +150,11 @@
 
 
 def wait_kernel(turns, source_ref, target_ref, sems):
-    rows = source_ref.shape[0] // turns
+    groups = 8
+    rows = source_ref.shape[0] // groups
 
     def turn(number, _):
-        window = pl.ds(pl.multiple_of(number * rows, rows), rows)
+        window = pl.ds(pl.multiple_of(number % groups * rows, rows), rows)
         copy = pltpu.make_async_copy(source_ref.at[window], target_ref.at[window], sems.at[0])
         copy.start()
         copy.wait()
@@ -223,7 +224,6 @@
     stream_shape = shape((tok_dev, model_width), BF16)
     table_shapes = (
         shape((blocks, slots, tok_dev), BF16),
-        shape((blocks, tok_dev, slots), BF16),
         shape((blocks, tok_dev, 128), F32),
         shape(ln_gain.shape, F32),
     )
@@ -284,7 +284,7 @@
     other = (tuple(tables(False, other_ids, other_gain)), other_router, tuple(other_weights))
 
     def layer(block, received, context):
-        (send, take, picked, gain), router_part, layer_weights = context
+        (send, picked, gain), router_part, layer_weights = context
         chosen = pick(block)
         normed, outgoing = kernel_call(
             enter_kernel,
@@ -308,7 +308,7 @@
             ),
         )(chosen, received, normed, incoming, picked, router_part, *layer_weights)
         returned = exchange(results, "expert").reshape(slots, model_width)
-        return chosen, base, gate, take, returned
+        return chosen, base, gate, send, returned
 
     def run(block, received, context):
         return kernel_call(leave_kernel, 5, stream_shape)(
@@ -353,7 +353,7 @@
         arrived,
         waiting,
     )
-    stream = lax.ppermute(stream, "section", around)
+    stream = keep(lax.ppermute(stream, "section", around))
 
     def chip(number, stream):
         place = section_index - 2 * number
@@ -373,7 +373,10 @@
             stream,
         )
         return lax.cond(
-            odd == 0, lambda stream: keep(lax.ppermute(stream, "section", even_ring)), keep, stream
+            (odd == 0) & (number < sections // 2 - 1),
+            lambda stream: keep(lax.ppermute(stream, "section", even_ring)),
+            keep,
+            stream,
         )
 
     stream = lax.fori_loop(1, sections // 2, chip, stream)

time: 328 us -> 323 us (0.985)
    all_to_all x5, blocking collectives: 176 us -> 173 us  [exchange(): return lax.all_to_all(rows, axis, split_axis=0, concat_axis=0, tiled=True)]
where the time goes in v2:
time: 323 us
  blocking collectives  173 us (54%)
  starting transfers between devices  107 us (33%)
  Pallas kernels  22 us (7%)
  waiting for transfers between devices  18.4 us (6%)
    all_to_all x5, blocking collectives, exchange(): return lax.all_to_all(rows, axis, split_axis=0, concat_axis=0, tiled=True)  173 us
    ppermute x3, starting transfers between devices, chip(): lax.ppermute(stream, 'section', odd_ring)  68.7 us
    ppermute x1, starting transfers between devices, body(): arrived = lax.ppermute(fresh, 'section', pair)  38.6 us
    ppermute x3, waiting for transfers between devices, chip(): lax.ppermute(stream, 'section', odd_ring)  14.2 us
    pallas_call x2, Pallas kernels, layer(): kernel_call(layer_kernel, 10, (shape(incoming.shape, BF16), shape((tok_de...  8.8 us
  transfers between devices with their start and end apart: 5, of which 5 were waited for; matrix products, arithmetic and copies ran while one was open for 0% of the time, Pallas kernels for 0%

profile of v2, /device:TPU:1, one launch (start us, length us, event | category | flops | bytes accessed | tf_op | source)
XLA Modules:
  0.0 322.6 jit_solution(2968148434453214534)
XLA Ops:
  0.0 1.1 shard_map.82
  1.2 38.6 %collective-permute-start.9 = (bf16[128,1024]{1,0:T(8,128)(2,1)S(1)}, bf16[128,1024]{1,0:T(8,128)(2,1)S(1)}, u32[]{:S(2)}, u32[]{:S(2)}) collective-permute-start(bf16[128,1024]{1,0:T(8,128)(2,1)S(1)} %get-tuple-element.987), channel_id=1, source_target_pairs={{0,16},{16,0},{32,32},{48,48},{64,64},{80,80},{96,96},{112,112},{1... | collective-permute-start | bytes 786440 | tf_op jit(solution)/shard_map/ppermute | solution.py:342
  39.8 1.1 collective-permute-done.9
  40.9 32.6 %conditional.11 = (bf16[128,1024]{1,0:T(8,128)(2,1)S(1)}) conditional(s32[]{:T(128)} %convert_element_type.46, bf16[128,1024]{1,0:T(8,128)(2,1)S(1)} %get-tuple-element.986, (bf16[128,1024]{1,0:T(8,128)(2,1)S(1)}, f32[1,1024]{1,0:T(1,128)S(1)}, bf16[2,256,128]{2,1,0:T(8,128)(2,1)S(1)}, f32[2,128,128]{2,1,0:T(8,128)S(1)}, bf16[32,1024]{1,0:T(8,128)(2,1)}, ...), branch_computations={%region_4.5_spmd, %region_5.6_spmd} | conditional | flops 23221225472 | bytes 173281472 | solution.py:349
  40.9 2.6 branch_1_fun.27.received_ref
  43.6 0.0 copy-start
  43.6 0.9 copy-done
  44.5 0.0 copy-start.3
  44.5 0.0 copy-start.8
  44.5 0.0 copy-start.13
  44.5 0.0 copy-start.28
  44.5 0.5 branch_1_fun.28
  45.1 12.1 %all_to_all.57.incoming_ref = bf16[16,16,1024]{2,1,0:T(8,128)(2,1)S(1)} all-to-all(bf16[16,16,1024]{2,1,0:T(8,128)(2,1)S(1)} %bitcast.30), channel_id=1, replica_groups=mesh['section'=8,'expert'=16] {'expert'}, dimensions={0} | all-to-all | bytes 1048576 | tf_op jit(solution)/shard_map/cond/branch_1_fun/all_to_all | solution.py:251
  57.2 0.0 copy-done.3
  57.2 0.0 copy-done.8
  57.2 0.0 copy-done.13
  57.2 0.0 copy-done.18
  57.2 0.0 copy-done.28
  57.2 3.9 %branch_1_fun.29 = (bf16[16,16,1024]{2,1,0:T(8,128)(2,1)S(1)}, f32[128,1024]{1,0:T(8,128)S(1)}, f32[128,128]{1,0:T(8,128)S(1)}) custom-call(s32[8,128]{1,0:T(8,128)S(1)} %broadcast_9_pick_ref.0.pick_ref, bf16[128,1024]{1,0:T(8,128)(2,1)S(1)} %copy-done, bf16[128,1024]{1,0:T(8,128)(2,1)S(1)} %get-tuple-element.587.normed_ref, ...), custom_call_target="tpu_custom_call" | custom-call | flops 3221225472 | bytes 27262976 | tf_op jit(solution)/shard_map/cond/branch_1_fun/pallas_call | solution.py:296
  61.1 11.8 %all_to_all.58 = bf16[16,16,1024]{2,1,0:T(8,128)(2,1)S(1)} all-to-all(bf16[16,16,1024]{2,1,0:T(8,128)(2,1)S(1)} %get-tuple-element.597), channel_id=1, replica_groups=mesh['section'=8,'expert'=16] {'expert'}, dimensions={0} | all-to-all | bytes 1048576 | tf_op jit(solution)/shard_map/cond/branch_1_fun/all_to_all | solution.py:251
  73.0 0.3 branch_1_fun.30
  73.5 0.0 collective-permute-start.10
  73.5 0.1 shard_map.84
  73.6 0.0 copy-start.25
  73.6 0.1 shard_map.85
  73.7 3.1 collective-permute-done.10.source_ref
  76.8 0.7 shard_map.83
  77.6 0.0 copy-done.25
  77.6 118.1 %while.20 = (s32[]{:T(128)}, bf16[128,1024]{1,0:T(8,128)(2,1)}, pred[]{:T(512)}, s32[]{:T(128)}, pred[]{:T(512)}, /*index=5*/s32[]{:T(128)}, f32[1,1024]{1,0:T(1...) while((s32[]{:T(128)}, bf16[128,1024]{1,0:T(8,128)(2,1)}, ...), condition=%wide.region_17.18_spmd, body=%wide.region_8.17_spmd.sunk | while | flops 46442450944 | bytes 346039136 | solution.py:382
  77.6 30.6 %conditional.18 = (bf16[128,1024]{1,0:T(8,128)(2,1)S(1)}) conditional(s32[]{:T(128)} %convert_element_type.56, bf16[128,1024]{1,0:T(8,128)(2,1)} %get-tuple-element.933, (s32[]{:T(128)}, bf16[128,1024]{1,0:T(8,128)(2,1)}, f32[1,1024]{1,0:T(1,128)S(1)}, bf16[2,256,128]{2,1,0:T(8,128)(2,1)S(1)}, f32[2,128,128]{2,1,0:T(8,128)S(1)}, ...), branch_computations={%region_9.9_spmd, %region_10.10_spmd} | conditional | flops 23221225472 | bytes 171970688 | solution.py:360
  77.6 0.0 copy-start.14
  77.6 0.0 copy-start.19
  77.6 1.6 branch_1_fun.31
  79.2 12.1 %all_to_all.59.incoming_ref = bf16[16,16,1024]{2,1,0:T(8,128)(2,1)S(1)} all-to-all(bf16[16,16,1024]{2,1,0:T(8,128)(2,1)S(1)} %bitcast.22), channel_id=1, replica_groups=mesh['section'=8,'expert'=16] {'expert'}, dimensions={0} | all-to-all | bytes 1048576 | tf_op jit(solution)/shard_map/while/body/eval_jaxpr/cond/branch_1_fun/all_to_all | solution.py:251
  91.4 0.0 copy-done.4
  91.4 0.0 copy-done.9
  91.4 0.0 copy-done.14
  91.4 0.0 copy-done.19
  91.4 4.9 %branch_1_fun.32 = (bf16[16,16,1024]{2,1,0:T(8,128)(2,1)S(1)}, f32[128,1024]{1,0:T(8,128)S(1)}, f32[128,128]{1,0:T(8,128)S(1)}) custom-call(s32[8,128]{1,0:T(8,128)S(1)} %broadcast_in_dim.4.pick_ref, bf16[128,1024]{1,0:T(8,128)(2,1)} %get-tuple-element.606.received_ref, bf16[128,1024]{1,0:T(8,128)(2,1)S(1)} %get-tuple-element.609.normed_ref, ...), custom_call_target="tpu_custom_call" | custom-call | flops 3221225472 | bytes 27262976 | tf_op jit(solution)/shard_map/while/body/eval_jaxpr/cond/branch_1_fun/pallas_call | solution.py:296
  96.3 11.6 %all_to_all.60 = bf16[16,16,1024]{2,1,0:T(8,128)(2,1)S(1)} all-to-all(bf16[16,16,1024]{2,1,0:T(8,128)(2,1)S(1)} %get-tuple-element.619), channel_id=1, replica_groups=mesh['section'=8,'expert'=16] {'expert'}, dimensions={0} | all-to-all | bytes 1048576 | tf_op jit(solution)/shard_map/while/body/eval_jaxpr/cond/branch_1_fun/all_to_all | solution.py:251
  107.9 0.3 branch_1_fun.33
  108.2 8.4 %conditional.19 = (bf16[128,1024]{1,0:T(8,128)(2,1)S(1)}) conditional(s32[]{:T(128)} %convert_element_type.55, bf16[128,1024]{1,0:T(8,128)(2,1)S(1)} %get-tuple-element.991, bf16[128,1024]{1,0:T(8,128)(2,1)S(1)} %get-tuple-element.991), branch_computations={%region_11.11_spmd, %region_12.12_spmd} | conditional | bytes 1048624 | solution.py:366
  108.2 1.9 collective-permute-start.7
  110.2 6.4 %collective-permute-done.7.source_ref = bf16[128,1024]{1,0:T(8,128)(2,1)S(1)} collective-permute-done((bf16[128,1024]{1,0:T(8,128)(2,1)S(1)}, bf16[128,1024]{1,0:T(8,128)(2,1)S(1)}, u32[]{:S(2)}, u32[]{:S(2)}) %collective-permute-start.7) | collective-permute-done | bytes 262176 | tf_op jit(solution)/shard_map/while/body/eval_jaxpr/cond/branch_1_fun/ppermute | solution.py:367
  116.7 0.7 conditional.21
  116.7 0.7 branch_0_fun.12
  117.4 1.0 conditional.18
  117.4 1.0 branch_0_fun.9
  118.4 66.3 %conditional.19 = (bf16[128,1024]{1,0:T(8,128)(2,1)S(1)}) conditional(s32[]{:T(128)} %convert_element_type.55, bf16[128,1024]{1,0:T(8,128)(2,1)S(1)} %get-tuple-element.991, bf16[128,1024]{1,0:T(8,128)(2,1)S(1)} %get-tuple-element.991), branch_computations={%region_11.11_spmd, %region_12.12_spmd} | conditional | bytes 1048624 | solution.py:366
  118.4 62.9 %collective-permute-start.7 = (bf16[128,1024]{1,0:T(8,128)(2,1)S(1)}, bf16[128,1024]{1,0:T(8,128)(2,1)S(1)}, u32[]{:S(2)}, u32[]{:S(2)}) collective-permute-start(bf16[128,1024]{1,0:T(8,128)(2,1)S(1)} %param.11), channel_id=1, source_target_pairs={{0,0},{32,32},{64,64},{96,96},{16,48},{48,80},{80,112},{112,16},{1... | collective-permute-start | bytes 786440 | tf_op jit(solution)/shard_map/while/body/eval_jaxpr/cond/branch_1_fun/ppermute | solution.py:367
  181.4 3.3 %collective-permute-done.7.source_ref = bf16[128,1024]{1,0:T(8,128)(2,1)S(1)} collective-permute-done((bf16[128,1024]{1,0:T(8,128)(2,1)S(1)}, bf16[128,1024]{1,0:T(8,128)(2,1)S(1)}, u32[]{:S(2)}, u32[]{:S(2)}) %collective-permute-start.7) | collective-permute-done | bytes 262176 | tf_op jit(solution)/shard_map/while/body/eval_jaxpr/cond/branch_1_fun/ppermute | solution.py:367
  184.7 0.7 conditional.21
  184.7 0.7 branch_0_fun.12
  185.5 1.0 conditional.18
  185.5 1.0 branch_0_fun.9
  186.5 8.4 %conditional.19 = (bf16[128,1024]{1,0:T(8,128)(2,1)S(1)}) conditional(s32[]{:T(128)} %convert_element_type.55, bf16[128,1024]{1,0:T(8,128)(2,1)S(1)} %get-tuple-element.991, bf16[128,1024]{1,0:T(8,128)(2,1)S(1)} %get-tuple-element.991), branch_computations={%region_11.11_spmd, %region_12.12_spmd} | conditional | bytes 1048624 | solution.py:366
  186.5 3.8 %collective-permute-start.7 = (bf16[128,1024]{1,0:T(8,128)(2,1)S(1)}, bf16[128,1024]{1,0:T(8,128)(2,1)S(1)}, u32[]{:S(2)}, u32[]{:S(2)}) collective-permute-start(bf16[128,1024]{1,0:T(8,128)(2,1)S(1)} %param.11), channel_id=1, source_target_pairs={{0,0},{32,32},{64,64},{96,96},{16,48},{48,80},{80,112},{112,16},{1... | collective-permute-start | bytes 786440 | tf_op jit(solution)/shard_map/while/body/eval_jaxpr/cond/branch_1_fun/ppermute | solution.py:367
  190.3 4.5 %collective-permute-done.7.source_ref = bf16[128,1024]{1,0:T(8,128)(2,1)S(1)} collective-permute-done((bf16[128,1024]{1,0:T(8,128)(2,1)S(1)}, bf16[128,1024]{1,0:T(8,128)(2,1)S(1)}, u32[]{:S(2)}, u32[]{:S(2)}) %collective-permute-start.7) | collective-permute-done | bytes 262176 | tf_op jit(solution)/shard_map/while/body/eval_jaxpr/cond/branch_1_fun/ppermute | solution.py:367
  194.9 0.7 conditional.21
  194.9 0.7 branch_0_fun.12
  195.6 1.3 conditional.13
  195.6 1.0 branch_0_fun.13
  196.9 125.0 %all_to_all.65.pieces_ref = bf16[8,128,128]{2,1,0:T(8,128)(2,1)S(1)} all-to-all(bf16[8,128,128]{2,1,0:T(8,128)(2,1)S(1)} %get-tuple-element.990), channel_id=1, replica_groups=mesh['section'=8,'expert'=16] {'section'}, dimensions={0} | all-to-all | bytes 524288 | tf_op jit(solution)/shard_map/all_to_all | solution.py:251
  322.0 0.6 shard_map.86
  (20 shorter events, 0.4 us)
Async XLA Ops:
  1.2 39.7 %collective-permute-start.9 = (bf16[128,1024]{1,0:T(8,128)(2,1)S(1)}, bf16[128,1024]{1,0:T(8,128)(2,1)S(1)}, u32[]{:S(2)}, u32[]{:S(2)}) collective-permute-start(bf16[128,1024]{1,0:T(8,128)(2,1)S(1)} %get-tuple-element.987), channel_id=1, source_target_pairs={{0,16},{16,0},{32,32},{48,48},{64,64},{80,80},{96,96},{112,112},{1... | collective-permute-start | bytes 786440 | tf_op jit(solution)/shard_map/ppermute | solution.py:342
  43.6 1.0 copy-start
  44.5 12.7 %copy-start.3 = (bf16[2,1024,2048]{2,1,0:T(8,128)(2,1)S(1)}, bf16[2,1024,2048]{2,1,0:T(8,128)(2,1)}, u32[]{:S(2)}) copy-start(bf16[2,1024,2048]{2,1,0:T(8,128)(2,1)} %get-tuple-element.593.expert_in_ref) | copy-start | bytes 25165828 | tf_op jit(solution)/shard_map/cond
  44.5 12.7 %copy-start.8 = (bf16[2,2048,1024]{2,1,0:T(8,128)(2,1)S(1)}, bf16[2,2048,1024]{2,1,0:T(8,128)(2,1)}, u32[]{:S(2)}) copy-start(bf16[2,2048,1024]{2,1,0:T(8,128)(2,1)} %get-tuple-element.594.expert_out_ref) | copy-start | bytes 25165828 | tf_op jit(solution)/shard_map/cond
  44.5 12.7 %copy-start.13 = (bf16[1024,2048]{1,0:T(8,128)(2,1)S(1)}, bf16[1024,2048]{1,0:T(8,128)(2,1)}, u32[]{:S(2)}) copy-start(bf16[1024,2048]{1,0:T(8,128)(2,1)} %get-tuple-element.591.dense_in_ref) | copy-start | bytes 12582916 | tf_op jit(solution)/shard_map/cond
  44.5 12.7 %copy-start.18 = (bf16[2048,1024]{1,0:T(8,128)(2,1)S(1)}, bf16[2048,1024]{1,0:T(8,128)(2,1)}, u32[]{:S(2)}) copy-start(bf16[2048,1024]{1,0:T(8,128)(2,1)} %get-tuple-element.592.dense_out_ref) | copy-start | bytes 12582916 | tf_op jit(solution)/shard_map/cond
  44.5 12.7 %copy-start.28 = (bf16[32,1024]{1,0:T(8,128)(2,1)S(1)}, bf16[32,1024]{1,0:T(8,128)(2,1)}, u32[]{:S(2)}) copy-start(bf16[32,1024]{1,0:T(8,128)(2,1)} %get-tuple-element.590.router_ref) | copy-start | bytes 196612 | tf_op jit(solution)/shard_map/cond
  73.5 3.3 %collective-permute-start.10 = (bf16[128,1024]{1,0:T(8,128)(2,1)S(1)}, bf16[128,1024]{1,0:T(8,128)(2,1)S(1)}, u32[]{:S(2)}, u32[]{:S(2)}) collective-permute-start(bf16[128,1024]{1,0:T(8,128)(2,1)S(1)} %get-tuple-element.988), channel_id=1, source_target_pairs={{0,16},{16,32},{32,48},{48,64},{64,80},{80,96},{96,112},{112,0},{1... | collective-permute-start | bytes 786440 | tf_op jit(solution)/shard_map/ppermute | solution.py:356
  73.6 4.0 %copy-start.25 = (bf16[1,1024,32]{1,2,0:T(8,128)(2,1)S(1)}, bf16[1,1024,32]{1,2,0:T(8,128)(2,1)}, u32[]{:S(2)}) copy-start(bf16[1,1024,32]{1,2,0:T(8,128)(2,1)} %param.30) | copy-start | bytes 196612
  77.6 13.8 %copy-start.4 = (bf16[2,1024,2048]{2,1,0:T(8,128)(2,1)S(1)}, bf16[2,1024,2048]{2,1,0:T(8,128)(2,1)}, u32[]{:S(2)}) copy-start(bf16[2,1024,2048]{2,1,0:T(8,128)(2,1)} %get-tuple-element.615.expert_in_ref) | copy-start | bytes 25165828 | tf_op jit(solution)/shard_map/while/body/eval_jaxpr/cond
  77.6 13.8 %copy-start.9 = (bf16[2,2048,1024]{2,1,0:T(8,128)(2,1)S(1)}, bf16[2,2048,1024]{2,1,0:T(8,128)(2,1)}, u32[]{:S(2)}) copy-start(bf16[2,2048,1024]{2,1,0:T(8,128)(2,1)} %get-tuple-element.616.expert_out_ref) | copy-start | bytes 25165828 | tf_op jit(solution)/shard_map/while/body/eval_jaxpr/cond
  77.6 13.8 %copy-start.14 = (bf16[1024,2048]{1,0:T(8,128)(2,1)S(1)}, bf16[1024,2048]{1,0:T(8,128)(2,1)}, u32[]{:S(2)}) copy-start(bf16[1024,2048]{1,0:T(8,128)(2,1)} %get-tuple-element.613.dense_in_ref) | copy-start | bytes 12582916 | tf_op jit(solution)/shard_map/while/body/eval_jaxpr/cond
  77.6 13.8 %copy-start.19 = (bf16[2048,1024]{1,0:T(8,128)(2,1)S(1)}, bf16[2048,1024]{1,0:T(8,128)(2,1)}, u32[]{:S(2)}) copy-start(bf16[2048,1024]{1,0:T(8,128)(2,1)} %get-tuple-element.614.dense_out_ref) | copy-start | bytes 12582916 | tf_op jit(solution)/shard_map/while/body/eval_jaxpr/cond
  108.2 8.3 %collective-permute-start.7 = (bf16[128,1024]{1,0:T(8,128)(2,1)S(1)}, bf16[128,1024]{1,0:T(8,128)(2,1)S(1)}, u32[]{:S(2)}, u32[]{:S(2)}) collective-permute-start(bf16[128,1024]{1,0:T(8,128)(2,1)S(1)} %param.11), channel_id=1, source_target_pairs={{0,0},{32,32},{64,64},{96,96},{16,48},{48,80},{80,112},{112,16},{1... | collective-permute-start | bytes 786440 | tf_op jit(solution)/shard_map/while/body/eval_jaxpr/cond/branch_1_fun/ppermute | solution.py:367
  118.4 66.2 %collective-permute-start.7 = (bf16[128,1024]{1,0:T(8,128)(2,1)S(1)}, bf16[128,1024]{1,0:T(8,128)(2,1)S(1)}, u32[]{:S(2)}, u32[]{:S(2)}) collective-permute-start(bf16[128,1024]{1,0:T(8,128)(2,1)S(1)} %param.11), channel_id=1, source_target_pairs={{0,0},{32,32},{64,64},{96,96},{16,48},{48,80},{80,112},{112,16},{1... | collective-permute-start | bytes 786440 | tf_op jit(solution)/shard_map/while/body/eval_jaxpr/cond/branch_1_fun/ppermute | solution.py:367
  186.5 8.3 %collective-permute-start.7 = (bf16[128,1024]{1,0:T(8,128)(2,1)S(1)}, bf16[128,1024]{1,0:T(8,128)(2,1)S(1)}, u32[]{:S(2)}, u32[]{:S(2)}) collective-permute-start(bf16[128,1024]{1,0:T(8,128)(2,1)S(1)} %param.11), channel_id=1, source_target_pairs={{0,0},{32,32},{64,64},{96,96},{16,48},{48,80},{80,112},{112,16},{1... | collective-permute-start | bytes 786440 | tf_op jit(solution)/shard_map/while/body/eval_jaxpr/cond/branch_1_fun/ppermute | solution.py:367

commit v3 on v2

--- a/solution.py
+++ b/solution.py
@@ -11,7 +11,7 @@
 F32 = jnp.float32
 VMEM_SPEC = pl.BlockSpec(memory_space=pltpu.VMEM)
 LIMIT = 30 << 20
-TURNS = 36
+TURNS = 22
 
 
 def dot(a, b):
@@ -70,7 +70,10 @@
     return jnp.where(second, table_ref[1].astype(F32), table_ref[0].astype(F32))
 
 
-def enter_kernel(pick_ref, received_ref, gain_ref, send_ref, normed_ref, outgoing_ref):
+def enter_kernel(
+    pick_ref, received_ref, gain_ref, send_ref, normed_ref, outgoing_ref, stream_ref
+):
+    stream_ref[...] = received_ref[...]
     stream = received_ref[...].astype(F32)
     centred = stream - jnp.mean(stream, axis=-1, keepdims=True)
     variance = jnp.mean(centred * centred, axis=-1, keepdims=True)
@@ -286,10 +289,10 @@
     def layer(block, received, context):
         (send, picked, gain), router_part, layer_weights = context
         chosen = pick(block)
-        normed, outgoing = kernel_call(
+        normed, outgoing, received = kernel_call(
             enter_kernel,
             4,
-            (stream_shape, shape((slots, model_width), BF16)),
+            (stream_shape, shape((slots, model_width), BF16), stream_shape),
             pl.CostEstimate(flops=20_000_000_000, transcendentals=0, bytes_accessed=40 << 20),
         )(chosen, received, gain, send)
         incoming = exchange(outgoing.reshape(members, slots // members, model_width), "expert")
@@ -327,11 +330,8 @@
             scratch_shapes=[pltpu.SemaphoreType.DMA((1,))],
         )(stream)
 
-    everyone = [(source, source) for source in range(sections)]
-    pair = [(0, 1), (1, 0)] + everyone[2:]
     around = [(source, (source + 1) % sections) for source in range(sections)]
-    odd_ring = everyone[0::2] + [(source, (source + 2) % sections) for source in range(1, sections, 2)]
-    even_ring = everyone[1::2] + [(source, (source + 2) % sections) for source in range(0, sections, 2)]
+    two_on = [(source, (source + 2) % sections) for source in range(sections)]
 
     fresh = lax.cond(
         section_index == 0,
@@ -339,7 +339,7 @@
         lambda stream: jnp.zeros((tok_dev, model_width), BF16),
         first,
     )
-    arrived = lax.ppermute(fresh, "section", pair)
+    arrived = lax.ppermute(fresh, "section", around)
     waiting = lax.cond(
         section_index == 0,
         lambda stream: run(1, stream, own),
@@ -353,10 +353,19 @@
         arrived,
         waiting,
     )
-    stream = keep(lax.ppermute(stream, "section", around))
+    stream = lax.ppermute(stream, "section", around)
 
     def chip(number, stream):
         place = section_index - 2 * number
+        stream = lax.switch(
+            jnp.where(odd == 1, 0, jnp.where(number > 1, 1, 2)),
+            (
+                keep,
+                lambda stream: keep(lax.ppermute(stream, "section", two_on)),
+                late_start,
+            ),
+            stream,
+        )
         stream = lax.cond(
             (place == -1) | (place == 0),
             lambda stream: run(own_block, stream, own),
@@ -364,7 +373,7 @@
             stream,
         )
         stream = lax.cond(
-            odd == 1, lambda stream: keep(lax.ppermute(stream, "section", odd_ring)), keep, stream
+            odd == 1, lambda stream: keep(lax.ppermute(stream, "section", two_on)), keep, stream
         )
         stream = lax.cond(
             (place == 0) | (place == 1),
@@ -372,12 +381,7 @@
             keep,
             stream,
         )
-        return lax.cond(
-            (odd == 0) & (number < sections // 2 - 1),
-            lambda stream: keep(lax.ppermute(stream, "section", even_ring)),
-            keep,
-            stream,
-        )
+        return stream
 
     stream = lax.fori_loop(1, sections // 2, chip, stream)
     pieces_shape = shape((sections, tok_dev, share), BF16)

time: 323 us -> 324 us (level)
    all_to_all x5, blocking collectives: 173 us -> 176 us  [exchange(): return lax.all_to_all(rows, axis, split_axis=0, concat_axis=0, tiled=True)]
where the time goes in v3:
time: 324 us
  blocking collectives  176 us (54%)
  starting transfers between devices  105 us (32%)
  waiting for transfers between devices  20.6 us (6%)
  Pallas kernels  19.4 us (6%)
    all_to_all x5, blocking collectives, exchange(): return lax.all_to_all(rows, axis, split_axis=0, concat_axis=0, tiled=True)  176 us
    ppermute x3, starting transfers between devices, chip(): lax.ppermute(stream, 'section', two_on)  61.6 us
    ppermute x1, starting transfers between devices, body(): arrived = lax.ppermute(fresh, 'section', around)  43.7 us
    ppermute x3, waiting for transfers between devices, chip(): lax.ppermute(stream, 'section', two_on)  14.3 us
    pallas_call x2, Pallas kernels, layer(): kernel_call(layer_kernel, 10, (shape(incoming.shape, BF16), shape((tok_de...  7.83 us
  transfers between devices with their start and end apart: 5, of which 5 were waited for; matrix products, arithmetic and copies ran while one was open for 0% of the time, Pallas kernels for 0%

profile of v3, /device:TPU:1, one launch (start us, length us, event | category | flops | bytes accessed | tf_op | source)
XLA Modules:
  0.0 324.0 jit_solution(5175946814778655214)
XLA Ops:
  0.0 1.1 shard_map.82
  1.2 43.7 %collective-permute-start.9 = (bf16[128,1024]{1,0:T(8,128)(2,1)S(1)}, bf16[128,1024]{1,0:T(8,128)(2,1)S(1)}, u32[]{:S(2)}, u32[]{:S(2)}) collective-permute-start(bf16[128,1024]{1,0:T(8,128)(2,1)S(1)} %get-tuple-element.983), channel_id=1, source_target_pairs={{0,16},{16,32},{32,48},{48,64},{64,80},{80,96},{96,112},{112,0},{1... | collective-permute-start | bytes 786440 | tf_op jit(solution)/shard_map/ppermute | solution.py:342
  44.9 3.3 %collective-permute-done.9 = bf16[128,1024]{1,0:T(8,128)(2,1)S(1)} collective-permute-done((bf16[128,1024]{1,0:T(8,128)(2,1)S(1)}, bf16[128,1024]{1,0:T(8,128)(2,1)S(1)}, u32[]{:S(2)}, u32[]{:S(2)}) %collective-permute-start.9) | collective-permute-done | bytes 262176 | tf_op jit(solution)/shard_map/ppermute | solution.py:342
  48.2 37.7 %conditional.11 = (bf16[128,1024]{1,0:T(8,128)(2,1)S(1)}) conditional(s32[]{:T(128)} %convert_element_type.38, bf16[128,1024]{1,0:T(8,128)(2,1)S(1)} %get-tuple-element.982, (bf16[128,1024]{1,0:T(8,128)(2,1)S(1)}, f32[1,1024]{1,0:T(1,128)S(1)}, bf16[2,256,128]{2,1,0:T(8,128)(2,1)S(1)}, f32[2,128,128]{2,1,0:T(8,128)S(1)}, bf16[32,1024]{1,0:T(8,128)(2,1)}, ...), branch_computations={%region_4.5_spmd, %region_5.6_spmd} | conditional | flops 23221225472 | bytes 173281472 | solution.py:349
  48.2 1.9 branch_1_fun.27.received_ref
  50.1 0.0 copy-start
  50.1 0.9 copy-done
  51.1 0.0 copy-start.28
  51.1 0.5 branch_1_fun.28
  51.6 17.8 %all_to_all.57.incoming_ref = bf16[16,16,1024]{2,1,0:T(8,128)(2,1)S(1)} all-to-all(bf16[16,16,1024]{2,1,0:T(8,128)(2,1)S(1)} %bitcast.28), channel_id=1, replica_groups=mesh['section'=8,'expert'=16] {'expert'}, dimensions={0} | all-to-all | bytes 1048576 | tf_op jit(solution)/shard_map/cond/branch_1_fun/all_to_all | solution.py:254
  69.4 0.0 copy-done.3
  69.4 0.0 copy-done.8
  69.5 0.0 copy-done.13
  69.5 0.0 copy-done.18
  69.5 0.0 copy-done.28
  69.5 3.9 %branch_1_fun.29 = (bf16[16,16,1024]{2,1,0:T(8,128)(2,1)S(1)}, f32[128,1024]{1,0:T(8,128)S(1)}, f32[128,128]{1,0:T(8,128)S(1)}) custom-call(s32[8,128]{1,0:T(8,128)S(1)} %broadcast_9_pick_ref.0.pick_ref, bf16[128,1024]{1,0:T(8,128)(2,1)S(1)} %get-tuple-element.594.received_ref, bf16[128,1024]{1,0:T(8,128)(2,1)S(1)} %get-tuple-element.595.normed_ref, ...), custom_call_target="tpu_custom_call" | custom-call | flops 3221225472 | bytes 27262976 | tf_op jit(solution)/shard_map/cond/branch_1_fun/pallas_call | solution.py:299
  73.4 12.1 %all_to_all.58 = bf16[16,16,1024]{2,1,0:T(8,128)(2,1)S(1)} all-to-all(bf16[16,16,1024]{2,1,0:T(8,128)(2,1)S(1)} %get-tuple-element.605), channel_id=1, replica_groups=mesh['section'=8,'expert'=16] {'expert'}, dimensions={0} | all-to-all | bytes 1048576 | tf_op jit(solution)/shard_map/cond/branch_1_fun/all_to_all | solution.py:254
  85.4 0.3 branch_1_fun.30
  86.0 0.0 collective-permute-start.10
  86.0 0.1 shard_map.83
  86.1 0.0 copy-start.25
  86.1 0.1 shard_map.84
  86.2 3.1 collective-permute-done.10
  89.3 0.0 copy-done.25
  89.3 109.9 %while.26 = (s32[]{:T(128)}, bf16[128,1024]{1,0:T(8,128)(2,1)}, s32[]{:T(128)}, pred[]{:T(512)}, s32[]{:T(128)}, /*index=5*/f32[1,1024]{1,0:T(1,128)S(1)}, bf16[...) while((s32[]{:T(128)}, bf16[128,1024]{1,0:T(8,128)(2,1)}, ...), condition=%wide.region_18.19_spmd, body=%wide.region_8.18_spmd.sunk | while | flops 46442450944 | bytes 346039104 | solution.py:386
  89.3 1.0 conditional.18
  89.3 1.0 branch_0_fun.9
  90.3 28.6 %conditional.19 = (bf16[128,1024]{1,0:T(8,128)(2,1)S(1)}) conditional(s32[]{:T(128)} %convert_element_type.46, bf16[128,1024]{1,0:T(8,128)(2,1)S(1)} %get-tuple-element.987, (s32[]{:T(128)}, bf16[128,1024]{1,0:T(8,128)(2,1)S(1)}, f32[1,1024]{1,0:T(1,128)S(1)}, bf16[2,256,128]{2,1,0:T(8,128)(2,1)S(1)}, f32[2,128,128]{2,1,0:T(8,128)S(1)}, ...), branch_computations={%region_12.12_spmd, %region_13.13_spmd} | conditional | flops 23221225472 | bytes 171970688 | solution.py:369
  90.3 0.0 copy-start.4
  90.4 0.0 copy-start.9
  90.4 0.0 copy-start.14
  90.4 0.0 copy-start.19
  90.4 0.5 branch_1_fun.32
  90.9 12.1 %all_to_all.59.incoming_ref = bf16[16,16,1024]{2,1,0:T(8,128)(2,1)S(1)} all-to-all(bf16[16,16,1024]{2,1,0:T(8,128)(2,1)S(1)} %bitcast.22), channel_id=1, replica_groups=mesh['section'=8,'expert'=16] {'expert'}, dimensions={0} | all-to-all | bytes 1048576 | tf_op jit(solution)/shard_map/while/body/eval_jaxpr/cond/branch_1_fun/all_to_all | solution.py:254
  103.1 0.0 copy-done.4
  103.1 0.0 copy-done.9
  103.1 0.0 copy-done.14
  103.1 0.0 copy-done.19
  103.1 3.9 %branch_1_fun.33 = (bf16[16,16,1024]{2,1,0:T(8,128)(2,1)S(1)}, f32[128,1024]{1,0:T(8,128)S(1)}, f32[128,128]{1,0:T(8,128)S(1)}) custom-call(s32[8,128]{1,0:T(8,128)S(1)} %broadcast_in_dim.4.pick_ref, bf16[128,1024]{1,0:T(8,128)(2,1)S(1)} %get-tuple-element.617.received_ref, bf16[128,1024]{1,0:T(8,128)(2,1)S(1)} %get-tuple-element.618.normed_ref, ...), custom_call_target="tpu_custom_call" | custom-call | flops 3221225472 | bytes 27262976 | tf_op jit(solution)/shard_map/while/body/eval_jaxpr/cond/branch_1_fun/pallas_call | solution.py:299
  107.0 11.6 %all_to_all.60 = bf16[16,16,1024]{2,1,0:T(8,128)(2,1)S(1)} all-to-all(bf16[16,16,1024]{2,1,0:T(8,128)(2,1)S(1)} %get-tuple-element.628), channel_id=1, replica_groups=mesh['section'=8,'expert'=16] {'expert'}, dimensions={0} | all-to-all | bytes 1048576 | tf_op jit(solution)/shard_map/while/body/eval_jaxpr/cond/branch_1_fun/all_to_all | solution.py:254
  118.6 0.3 branch_1_fun.34
  119.0 6.5 %conditional.20 = (bf16[128,1024]{1,0:T(8,128)(2,1)S(1)}) conditional(s32[]{:T(128)} %convert_element_type.45, bf16[128,1024]{1,0:T(8,128)(2,1)S(1)} %get-tuple-element.988, bf16[128,1024]{1,0:T(8,128)(2,1)S(1)} %get-tuple-element.988), branch_computations={%region_14.14_spmd, %region_15.15_spmd} | conditional | bytes 1048624 | solution.py:375
  119.0 0.1 collective-permute-start.8
  119.1 6.4 %collective-permute-done.8.source_ref = bf16[128,1024]{1,0:T(8,128)(2,1)S(1)} collective-permute-done((bf16[128,1024]{1,0:T(8,128)(2,1)S(1)}, bf16[128,1024]{1,0:T(8,128)(2,1)S(1)}, u32[]{:S(2)}, u32[]{:S(2)}) %collective-permute-start.8) | collective-permute-done | bytes 262176 | tf_op jit(solution)/shard_map/while/body/eval_jaxpr/cond/branch_1_fun/ppermute | solution.py:376
  125.5 0.7 conditional.21
  125.5 0.7 branch_0_fun.12
  126.2 1.0 conditional.18
  126.2 1.0 branch_0_fun.9
  127.3 62.9 %conditional.20 = (bf16[128,1024]{1,0:T(8,128)(2,1)S(1)}) conditional(s32[]{:T(128)} %convert_element_type.45, bf16[128,1024]{1,0:T(8,128)(2,1)S(1)} %get-tuple-element.988, bf16[128,1024]{1,0:T(8,128)(2,1)S(1)} %get-tuple-element.988), branch_computations={%region_14.14_spmd, %region_15.15_spmd} | conditional | bytes 1048624 | solution.py:375
  127.3 59.5 %collective-permute-start.8 = (bf16[128,1024]{1,0:T(8,128)(2,1)S(1)}, bf16[128,1024]{1,0:T(8,128)(2,1)S(1)}, u32[]{:S(2)}, u32[]{:S(2)}) collective-permute-start(bf16[128,1024]{1,0:T(8,128)(2,1)S(1)} %param.14), channel_id=1, source_target_pairs={{0,32},{16,48},{32,64},{48,80},{64,96},{80,112},{96,0},{112,16},{1... | collective-permute-start | bytes 786440 | tf_op jit(solution)/shard_map/while/body/eval_jaxpr/cond/branch_1_fun/ppermute | solution.py:376
  186.8 3.3 %collective-permute-done.8.source_ref = bf16[128,1024]{1,0:T(8,128)(2,1)S(1)} collective-permute-done((bf16[128,1024]{1,0:T(8,128)(2,1)S(1)}, bf16[128,1024]{1,0:T(8,128)(2,1)S(1)}, u32[]{:S(2)}, u32[]{:S(2)}) %collective-permute-start.8) | collective-permute-done | bytes 262176 | tf_op jit(solution)/shard_map/while/body/eval_jaxpr/cond/branch_1_fun/ppermute | solution.py:376
  190.2 0.7 conditional.21
  190.2 0.7 branch_0_fun.12
  190.9 1.0 conditional.18
  190.9 1.0 branch_0_fun.9
  191.9 6.5 %conditional.20 = (bf16[128,1024]{1,0:T(8,128)(2,1)S(1)}) conditional(s32[]{:T(128)} %convert_element_type.45, bf16[128,1024]{1,0:T(8,128)(2,1)S(1)} %get-tuple-element.988, bf16[128,1024]{1,0:T(8,128)(2,1)S(1)} %get-tuple-element.988), branch_computations={%region_14.14_spmd, %region_15.15_spmd} | conditional | bytes 1048624 | solution.py:375
  192.0 2.0 collective-permute-start.8
  193.9 4.5 %collective-permute-done.8.source_ref = bf16[128,1024]{1,0:T(8,128)(2,1)S(1)} collective-permute-done((bf16[128,1024]{1,0:T(8,128)(2,1)S(1)}, bf16[128,1024]{1,0:T(8,128)(2,1)S(1)}, u32[]{:S(2)}, u32[]{:S(2)}) %collective-permute-start.8) | collective-permute-done | bytes 262176 | tf_op jit(solution)/shard_map/while/body/eval_jaxpr/cond/branch_1_fun/ppermute | solution.py:376
  198.5 0.7 conditional.21
  198.5 0.7 branch_0_fun.12
  199.2 1.3 conditional.13
  199.2 1.0 branch_0_fun.13
  200.5 122.8 %all_to_all.65.pieces_ref = bf16[8,128,128]{2,1,0:T(8,128)(2,1)S(1)} all-to-all(bf16[8,128,128]{2,1,0:T(8,128)(2,1)S(1)} %get-tuple-element.986), channel_id=1, replica_groups=mesh['section'=8,'expert'=16] {'section'}, dimensions={0} | all-to-all | bytes 524288 | tf_op jit(solution)/shard_map/all_to_all | solution.py:254
  323.3 0.6 shard_map.85
  (19 shorter events, 0.3 us)
Async XLA Ops:
  1.2 47.0 %collective-permute-start.9 = (bf16[128,1024]{1,0:T(8,128)(2,1)S(1)}, bf16[128,1024]{1,0:T(8,128)(2,1)S(1)}, u32[]{:S(2)}, u32[]{:S(2)}) collective-permute-start(bf16[128,1024]{1,0:T(8,128)(2,1)S(1)} %get-tuple-element.983), channel_id=1, source_target_pairs={{0,16},{16,32},{32,48},{48,64},{64,80},{80,96},{96,112},{112,0},{1... | collective-permute-start | bytes 786440 | tf_op jit(solution)/shard_map/ppermute | solution.py:342
  50.1 1.0 copy-start
  51.1 18.4 %copy-start.3 = (bf16[2,1024,2048]{2,1,0:T(8,128)(2,1)S(1)}, bf16[2,1024,2048]{2,1,0:T(8,128)(2,1)}, u32[]{:S(2)}) copy-start(bf16[2,1024,2048]{2,1,0:T(8,128)(2,1)} %get-tuple-element.601.expert_in_ref) | copy-start | bytes 25165828 | tf_op jit(solution)/shard_map/cond
  51.1 18.4 %copy-start.8 = (bf16[2,2048,1024]{2,1,0:T(8,128)(2,1)S(1)}, bf16[2,2048,1024]{2,1,0:T(8,128)(2,1)}, u32[]{:S(2)}) copy-start(bf16[2,2048,1024]{2,1,0:T(8,128)(2,1)} %get-tuple-element.602.expert_out_ref) | copy-start | bytes 25165828 | tf_op jit(solution)/shard_map/cond
  51.1 18.4 %copy-start.13 = (bf16[1024,2048]{1,0:T(8,128)(2,1)S(1)}, bf16[1024,2048]{1,0:T(8,128)(2,1)}, u32[]{:S(2)}) copy-start(bf16[1024,2048]{1,0:T(8,128)(2,1)} %get-tuple-element.599.dense_in_ref) | copy-start | bytes 12582916 | tf_op jit(solution)/shard_map/cond
  51.1 18.4 %copy-start.18 = (bf16[2048,1024]{1,0:T(8,128)(2,1)S(1)}, bf16[2048,1024]{1,0:T(8,128)(2,1)}, u32[]{:S(2)}) copy-start(bf16[2048,1024]{1,0:T(8,128)(2,1)} %get-tuple-element.600.dense_out_ref) | copy-start | bytes 12582916 | tf_op jit(solution)/shard_map/cond
  51.1 18.4 %copy-start.28 = (bf16[32,1024]{1,0:T(8,128)(2,1)S(1)}, bf16[32,1024]{1,0:T(8,128)(2,1)}, u32[]{:S(2)}) copy-start(bf16[32,1024]{1,0:T(8,128)(2,1)} %get-tuple-element.598.router_ref) | copy-start | bytes 196612 | tf_op jit(solution)/shard_map/cond
  86.0 3.3 %collective-permute-start.10 = (bf16[128,1024]{1,0:T(8,128)(2,1)S(1)}, bf16[128,1024]{1,0:T(8,128)(2,1)}, u32[]{:S(2)}, u32[]{:S(2)}) collective-permute-start(bf16[128,1024]{1,0:T(8,128)(2,1)S(1)} %get-tuple-element.984), channel_id=1, source_target_pairs={{0,16},{16,32},{32,48},{48,64},{64,80},{80,96},{96,112},{112,0},{1... | collective-permute-start | bytes 786440 | tf_op jit(solution)/shard_map/ppermute | solution.py:356
  86.1 3.2 copy-start.25
  90.3 12.7 %copy-start.4 = (bf16[2,1024,2048]{2,1,0:T(8,128)(2,1)S(1)}, bf16[2,1024,2048]{2,1,0:T(8,128)(2,1)}, u32[]{:S(2)}) copy-start(bf16[2,1024,2048]{2,1,0:T(8,128)(2,1)} %get-tuple-element.624.expert_in_ref) | copy-start | bytes 25165828 | tf_op jit(solution)/shard_map/while/body/eval_jaxpr/cond
  90.4 12.7 %copy-start.9 = (bf16[2,2048,1024]{2,1,0:T(8,128)(2,1)S(1)}, bf16[2,2048,1024]{2,1,0:T(8,128)(2,1)}, u32[]{:S(2)}) copy-start(bf16[2,2048,1024]{2,1,0:T(8,128)(2,1)} %get-tuple-element.625.expert_out_ref) | copy-start | bytes 25165828 | tf_op jit(solution)/shard_map/while/body/eval_jaxpr/cond
  90.4 12.7 %copy-start.14 = (bf16[1024,2048]{1,0:T(8,128)(2,1)S(1)}, bf16[1024,2048]{1,0:T(8,128)(2,1)}, u32[]{:S(2)}) copy-start(bf16[1024,2048]{1,0:T(8,128)(2,1)} %get-tuple-element.622.dense_in_ref) | copy-start | bytes 12582916 | tf_op jit(solution)/shard_map/while/body/eval_jaxpr/cond
  90.4 12.7 %copy-start.19 = (bf16[2048,1024]{1,0:T(8,128)(2,1)S(1)}, bf16[2048,1024]{1,0:T(8,128)(2,1)}, u32[]{:S(2)}) copy-start(bf16[2048,1024]{1,0:T(8,128)(2,1)} %get-tuple-element.623.dense_out_ref) | copy-start | bytes 12582916 | tf_op jit(solution)/shard_map/while/body/eval_jaxpr/cond
  119.0 6.5 %collective-permute-start.8 = (bf16[128,1024]{1,0:T(8,128)(2,1)S(1)}, bf16[128,1024]{1,0:T(8,128)(2,1)S(1)}, u32[]{:S(2)}, u32[]{:S(2)}) collective-permute-start(bf16[128,1024]{1,0:T(8,128)(2,1)S(1)} %param.14), channel_id=1, source_target_pairs={{0,32},{16,48},{32,64},{48,80},{64,96},{80,112},{96,0},{112,16},{1... | collective-permute-start | bytes 786440 | tf_op jit(solution)/shard_map/while/body/eval_jaxpr/cond/branch_1_fun/ppermute | solution.py:376
  127.3 62.8 %collective-permute-start.8 = (bf16[128,1024]{1,0:T(8,128)(2,1)S(1)}, bf16[128,1024]{1,0:T(8,128)(2,1)S(1)}, u32[]{:S(2)}, u32[]{:S(2)}) collective-permute-start(bf16[128,1024]{1,0:T(8,128)(2,1)S(1)} %param.14), channel_id=1, source_target_pairs={{0,32},{16,48},{32,64},{48,80},{64,96},{80,112},{96,0},{112,16},{1... | collective-permute-start | bytes 786440 | tf_op jit(solution)/shard_map/while/body/eval_jaxpr/cond/branch_1_fun/ppermute | solution.py:376
  192.0 6.5 %collective-permute-start.8 = (bf16[128,1024]{1,0:T(8,128)(2,1)S(1)}, bf16[128,1024]{1,0:T(8,128)(2,1)S(1)}, u32[]{:S(2)}, u32[]{:S(2)}) collective-permute-start(bf16[128,1024]{1,0:T(8,128)(2,1)S(1)} %param.14), channel_id=1, source_target_pairs={{0,32},{16,48},{32,64},{48,80},{64,96},{80,112},{96,0},{112,16},{1... | collective-permute-start | bytes 786440 | tf_op jit(solution)/shard_map/while/body/eval_jaxpr/cond/branch_1_fun/ppermute | solution.py:376

commit v4 on v3

--- a/solution.py
+++ b/solution.py
@@ -11,7 +11,8 @@
 F32 = jnp.float32
 VMEM_SPEC = pl.BlockSpec(memory_space=pltpu.VMEM)
 LIMIT = 30 << 20
-TURNS = 22
+FIRST_TURNS = 22
+SECOND_TURNS = 50
 
 
 def dot(a, b):
@@ -321,9 +322,9 @@
     def keep(stream):
         return kernel_call(keep_kernel, 1, stream_shape)(stream)
 
-    def late_start(stream):
+    def late_start(turns, stream):
         return pl.pallas_call(
-            functools.partial(wait_kernel, TURNS),
+            functools.partial(wait_kernel, turns),
             out_shape=stream_shape,
             in_specs=[VMEM_SPEC],
             out_specs=VMEM_SPEC,
@@ -331,6 +332,7 @@
         )(stream)
 
     around = [(source, (source + 1) % sections) for source in range(sections)]
+    first_pair = [(0, 1), (1, 0)] + [(source, source) for source in range(2, sections)]
     two_on = [(source, (source + 2) % sections) for source in range(sections)]
 
     fresh = lax.cond(
@@ -339,7 +341,7 @@
         lambda stream: jnp.zeros((tok_dev, model_width), BF16),
         first,
     )
-    arrived = lax.ppermute(fresh, "section", around)
+    arrived = lax.ppermute(fresh, "section", first_pair)
     waiting = lax.cond(
         section_index == 0,
         lambda stream: run(1, stream, own),
@@ -348,7 +350,7 @@
     )
     stream = lax.cond(
         section_index == 1,
-        lambda arrived, waiting: run(0, late_start(arrived), own),
+        lambda arrived, waiting: run(0, late_start(FIRST_TURNS, arrived), own),
         lambda arrived, waiting: keep(waiting),
         arrived,
         waiting,
@@ -362,7 +364,7 @@
             (
                 keep,
                 lambda stream: keep(lax.ppermute(stream, "section", two_on)),
-                late_start,
+                functools.partial(late_start, SECOND_TURNS),
             ),
             stream,
         )

time: 324 us -> 314 us (0.969)
  starting transfers between devices: 105 us -> 97.5 us
    ppermute x1, starting transfers between devices: 43.7 us -> 38.6 us  [body(): arrived = lax.ppermute(fresh, 'section', first_pair)]
where the time goes in v4:
time: 314 us; the launch traced here: 313 us
  blocking collectives  176 us (56%)
  starting transfers between devices  97.5 us (31%)
  Pallas kernels  19.4 us (6%)
  waiting for transfers between devices  18.4 us (6%)
    all_to_all x5, blocking collectives, exchange(): return lax.all_to_all(rows, axis, split_axis=0, concat_axis=0, tiled=True)  176 us
    ppermute x3, starting transfers between devices, chip(): lax.ppermute(stream, 'section', two_on)  58.9 us
    ppermute x1, starting transfers between devices, body(): arrived = lax.ppermute(fresh, 'section', first_pair)  38.6 us
    ppermute x3, waiting for transfers between devices, chip(): lax.ppermute(stream, 'section', two_on)  14.3 us
    pallas_call x2, Pallas kernels, layer(): kernel_call(layer_kernel, 10, (shape(incoming.shape, BF16), shape((tok_de...  7.84 us
  transfers between devices with their start and end apart: 5, of which 5 were waited for; matrix products, arithmetic and copies ran while one was open for 0% of the time, Pallas kernels for 0%

profile of v4, /device:TPU:1, one launch (start us, length us, event | category | flops | bytes accessed | tf_op | source)
XLA Modules:
  0.0 313.3 jit_solution(6188249232392647334)
XLA Ops:
  0.0 1.1 shard_map.82
  1.2 38.6 %collective-permute-start.9 = (bf16[128,1024]{1,0:T(8,128)(2,1)S(1)}, bf16[128,1024]{1,0:T(8,128)(2,1)S(1)}, u32[]{:S(2)}, u32[]{:S(2)}) collective-permute-start(bf16[128,1024]{1,0:T(8,128)(2,1)S(1)} %get-tuple-element.983), channel_id=1, source_target_pairs={{0,16},{16,0},{32,32},{48,48},{64,64},{80,80},{96,96},{112,112},{1... | collective-permute-start | bytes 786440 | tf_op jit(solution)/shard_map/ppermute | solution.py:344
  39.8 1.1 collective-permute-done.9
  40.9 32.5 %conditional.11 = (bf16[128,1024]{1,0:T(8,128)(2,1)S(1)}) conditional(s32[]{:T(128)} %convert_element_type.38, bf16[128,1024]{1,0:T(8,128)(2,1)S(1)} %get-tuple-element.982, (bf16[128,1024]{1,0:T(8,128)(2,1)S(1)}, f32[1,1024]{1,0:T(1,128)S(1)}, bf16[2,256,128]{2,1,0:T(8,128)(2,1)S(1)}, f32[2,128,128]{2,1,0:T(8,128)S(1)}, bf16[32,1024]{1,0:T(8,128)(2,1)}, ...), branch_computations={%region_4.5_spmd, %region_5.6_spmd} | conditional | flops 23221225472 | bytes 173281472 | solution.py:351
  40.9 1.9 branch_1_fun.27.received_ref
  42.8 0.0 copy-start
  42.8 0.9 copy-done
  43.7 0.0 copy-start.28
  43.8 0.5 branch_1_fun.28
  44.3 12.1 %all_to_all.57.incoming_ref = bf16[16,16,1024]{2,1,0:T(8,128)(2,1)S(1)} all-to-all(bf16[16,16,1024]{2,1,0:T(8,128)(2,1)S(1)} %bitcast.28), channel_id=1, replica_groups=mesh['section'=8,'expert'=16] {'expert'}, dimensions={0} | all-to-all | bytes 1048576 | tf_op jit(solution)/shard_map/cond/branch_1_fun/all_to_all | solution.py:255
  56.4 0.0 copy-done.3
  56.4 0.0 copy-done.8
  56.4 0.0 copy-done.13
  56.4 0.0 copy-done.18
  56.4 0.0 copy-done.28
  56.5 3.9 %branch_1_fun.29 = (bf16[16,16,1024]{2,1,0:T(8,128)(2,1)S(1)}, f32[128,1024]{1,0:T(8,128)S(1)}, f32[128,128]{1,0:T(8,128)S(1)}) custom-call(s32[8,128]{1,0:T(8,128)S(1)} %broadcast_9_pick_ref.0.pick_ref, bf16[128,1024]{1,0:T(8,128)(2,1)S(1)} %get-tuple-element.594.received_ref, bf16[128,1024]{1,0:T(8,128)(2,1)S(1)} %get-tuple-element.595.normed_ref, ...), custom_call_target="tpu_custom_call" | custom-call | flops 3221225472 | bytes 27262976 | tf_op jit(solution)/shard_map/cond/branch_1_fun/pallas_call | solution.py:300
  60.4 12.5 %all_to_all.58 = bf16[16,16,1024]{2,1,0:T(8,128)(2,1)S(1)} all-to-all(bf16[16,16,1024]{2,1,0:T(8,128)(2,1)S(1)} %get-tuple-element.605), channel_id=1, replica_groups=mesh['section'=8,'expert'=16] {'expert'}, dimensions={0} | all-to-all | bytes 1048576 | tf_op jit(solution)/shard_map/cond/branch_1_fun/all_to_all | solution.py:255
  72.9 0.3 branch_1_fun.30
  73.5 0.0 collective-permute-start.10
  73.5 0.1 shard_map.83
  73.6 0.0 copy-start.25
  73.6 0.1 shard_map.84
  73.7 3.1 collective-permute-done.10
  76.8 0.0 copy-done.25
  76.8 107.2 %while.26 = (s32[]{:T(128)}, bf16[128,1024]{1,0:T(8,128)(2,1)}, s32[]{:T(128)}, pred[]{:T(512)}, s32[]{:T(128)}, /*index=5*/f32[1,1024]{1,0:T(1,128)S(1)}, bf16[...) while((s32[]{:T(128)}, bf16[128,1024]{1,0:T(8,128)(2,1)}, ...), condition=%wide.region_18.19_spmd, body=%wide.region_8.18_spmd.sunk | while | flops 46442450944 | bytes 346039104 | solution.py:388
  76.8 1.0 conditional.18
  76.8 1.0 branch_0_fun.9
  77.8 28.6 %conditional.19 = (bf16[128,1024]{1,0:T(8,128)(2,1)S(1)}) conditional(s32[]{:T(128)} %convert_element_type.46, bf16[128,1024]{1,0:T(8,128)(2,1)S(1)} %get-tuple-element.987, (s32[]{:T(128)}, bf16[128,1024]{1,0:T(8,128)(2,1)S(1)}, f32[1,1024]{1,0:T(1,128)S(1)}, bf16[2,256,128]{2,1,0:T(8,128)(2,1)S(1)}, f32[2,128,128]{2,1,0:T(8,128)S(1)}, ...), branch_computations={%region_12.12_spmd, %region_13.13_spmd} | conditional | flops 23221225472 | bytes 171970688 | solution.py:371
  77.8 0.0 copy-start.4
  77.8 0.0 copy-start.9
  77.8 0.0 copy-start.14
  77.9 0.0 copy-start.19
  77.9 0.5 branch_1_fun.32
  78.4 12.1 %all_to_all.59.incoming_ref = bf16[16,16,1024]{2,1,0:T(8,128)(2,1)S(1)} all-to-all(bf16[16,16,1024]{2,1,0:T(8,128)(2,1)S(1)} %bitcast.22), channel_id=1, replica_groups=mesh['section'=8,'expert'=16] {'expert'}, dimensions={0} | all-to-all | bytes 1048576 | tf_op jit(solution)/shard_map/while/body/eval_jaxpr/cond/branch_1_fun/all_to_all | solution.py:255
  90.5 0.0 copy-done.4
  90.5 0.0 copy-done.9
  90.5 0.0 copy-done.14
  90.5 0.0 copy-done.19
  90.6 3.9 %branch_1_fun.33 = (bf16[16,16,1024]{2,1,0:T(8,128)(2,1)S(1)}, f32[128,1024]{1,0:T(8,128)S(1)}, f32[128,128]{1,0:T(8,128)S(1)}) custom-call(s32[8,128]{1,0:T(8,128)S(1)} %broadcast_in_dim.4.pick_ref, bf16[128,1024]{1,0:T(8,128)(2,1)S(1)} %get-tuple-element.617.received_ref, bf16[128,1024]{1,0:T(8,128)(2,1)S(1)} %get-tuple-element.618.normed_ref, ...), custom_call_target="tpu_custom_call" | custom-call | flops 3221225472 | bytes 27262976 | tf_op jit(solution)/shard_map/while/body/eval_jaxpr/cond/branch_1_fun/pallas_call | solution.py:300
  94.5 11.6 %all_to_all.60 = bf16[16,16,1024]{2,1,0:T(8,128)(2,1)S(1)} all-to-all(bf16[16,16,1024]{2,1,0:T(8,128)(2,1)S(1)} %get-tuple-element.628), channel_id=1, replica_groups=mesh['section'=8,'expert'=16] {'expert'}, dimensions={0} | all-to-all | bytes 1048576 | tf_op jit(solution)/shard_map/while/body/eval_jaxpr/cond/branch_1_fun/all_to_all | solution.py:255
  106.1 0.3 branch_1_fun.34
  106.4 6.5 %conditional.20 = (bf16[128,1024]{1,0:T(8,128)(2,1)S(1)}) conditional(s32[]{:T(128)} %convert_element_type.45, bf16[128,1024]{1,0:T(8,128)(2,1)S(1)} %get-tuple-element.988, bf16[128,1024]{1,0:T(8,128)(2,1)S(1)} %get-tuple-element.988), branch_computations={%region_14.14_spmd, %region_15.15_spmd} | conditional | bytes 1048624 | solution.py:377
  106.5 0.1 collective-permute-start.8
  106.5 6.4 %collective-permute-done.8.source_ref = bf16[128,1024]{1,0:T(8,128)(2,1)S(1)} collective-permute-done((bf16[128,1024]{1,0:T(8,128)(2,1)S(1)}, bf16[128,1024]{1,0:T(8,128)(2,1)S(1)}, u32[]{:S(2)}, u32[]{:S(2)}) %collective-permute-start.8) | collective-permute-done | bytes 262176 | tf_op jit(solution)/shard_map/while/body/eval_jaxpr/cond/branch_1_fun/ppermute | solution.py:378
  113.0 0.7 conditional.21
  113.0 0.7 branch_0_fun.12
  113.7 1.0 conditional.18
  113.7 1.0 branch_0_fun.9
  114.8 60.2 %conditional.20 = (bf16[128,1024]{1,0:T(8,128)(2,1)S(1)}) conditional(s32[]{:T(128)} %convert_element_type.45, bf16[128,1024]{1,0:T(8,128)(2,1)S(1)} %get-tuple-element.988, bf16[128,1024]{1,0:T(8,128)(2,1)S(1)} %get-tuple-element.988), branch_computations={%region_14.14_spmd, %region_15.15_spmd} | conditional | bytes 1048624 | solution.py:377
  114.8 56.8 %collective-permute-start.8 = (bf16[128,1024]{1,0:T(8,128)(2,1)S(1)}, bf16[128,1024]{1,0:T(8,128)(2,1)S(1)}, u32[]{:S(2)}, u32[]{:S(2)}) collective-permute-start(bf16[128,1024]{1,0:T(8,128)(2,1)S(1)} %param.14), channel_id=1, source_target_pairs={{0,32},{16,48},{32,64},{48,80},{64,96},{80,112},{96,0},{112,16},{1... | collective-permute-start | bytes 786440 | tf_op jit(solution)/shard_map/while/body/eval_jaxpr/cond/branch_1_fun/ppermute | solution.py:378
  171.6 3.3 %collective-permute-done.8.source_ref = bf16[128,1024]{1,0:T(8,128)(2,1)S(1)} collective-permute-done((bf16[128,1024]{1,0:T(8,128)(2,1)S(1)}, bf16[128,1024]{1,0:T(8,128)(2,1)S(1)}, u32[]{:S(2)}, u32[]{:S(2)}) %collective-permute-start.8) | collective-permute-done | bytes 262176 | tf_op jit(solution)/shard_map/while/body/eval_jaxpr/cond/branch_1_fun/ppermute | solution.py:378
  174.9 0.7 conditional.21
  175.0 0.7 branch_0_fun.12
  175.7 1.0 conditional.18
  175.7 1.0 branch_0_fun.9
  176.7 6.5 %conditional.20 = (bf16[128,1024]{1,0:T(8,128)(2,1)S(1)}) conditional(s32[]{:T(128)} %convert_element_type.45, bf16[128,1024]{1,0:T(8,128)(2,1)S(1)} %get-tuple-element.988, bf16[128,1024]{1,0:T(8,128)(2,1)S(1)} %get-tuple-element.988), branch_computations={%region_14.14_spmd, %region_15.15_spmd} | conditional | bytes 1048624 | solution.py:377
  176.7 2.0 collective-permute-start.8
  178.7 4.5 %collective-permute-done.8.source_ref = bf16[128,1024]{1,0:T(8,128)(2,1)S(1)} collective-permute-done((bf16[128,1024]{1,0:T(8,128)(2,1)S(1)}, bf16[128,1024]{1,0:T(8,128)(2,1)S(1)}, u32[]{:S(2)}, u32[]{:S(2)}) %collective-permute-start.8) | collective-permute-done | bytes 262176 | tf_op jit(solution)/shard_map/while/body/eval_jaxpr/cond/branch_1_fun/ppermute | solution.py:378
  183.3 0.7 conditional.21
  183.3 0.7 branch_0_fun.12
  184.0 1.3 conditional.13
  184.0 1.0 branch_0_fun.13
  185.3 127.4 %all_to_all.65.pieces_ref = bf16[8,128,128]{2,1,0:T(8,128)(2,1)S(1)} all-to-all(bf16[8,128,128]{2,1,0:T(8,128)(2,1)S(1)} %get-tuple-element.986), channel_id=1, replica_groups=mesh['section'=8,'expert'=16] {'section'}, dimensions={0} | all-to-all | bytes 524288 | tf_op jit(solution)/shard_map/all_to_all | solution.py:255
  312.7 0.6 shard_map.85
  (19 shorter events, 0.3 us)
Async XLA Ops:
  1.2 39.7 %collective-permute-start.9 = (bf16[128,1024]{1,0:T(8,128)(2,1)S(1)}, bf16[128,1024]{1,0:T(8,128)(2,1)S(1)}, u32[]{:S(2)}, u32[]{:S(2)}) collective-permute-start(bf16[128,1024]{1,0:T(8,128)(2,1)S(1)} %get-tuple-element.983), channel_id=1, source_target_pairs={{0,16},{16,0},{32,32},{48,48},{64,64},{80,80},{96,96},{112,112},{1... | collective-permute-start | bytes 786440 | tf_op jit(solution)/shard_map/ppermute | solution.py:344
  42.8 1.0 copy-start
  43.7 12.7 %copy-start.3 = (bf16[2,1024,2048]{2,1,0:T(8,128)(2,1)S(1)}, bf16[2,1024,2048]{2,1,0:T(8,128)(2,1)}, u32[]{:S(2)}) copy-start(bf16[2,1024,2048]{2,1,0:T(8,128)(2,1)} %get-tuple-element.601.expert_in_ref) | copy-start | bytes 25165828 | tf_op jit(solution)/shard_map/cond
  43.7 12.7 %copy-start.8 = (bf16[2,2048,1024]{2,1,0:T(8,128)(2,1)S(1)}, bf16[2,2048,1024]{2,1,0:T(8,128)(2,1)}, u32[]{:S(2)}) copy-start(bf16[2,2048,1024]{2,1,0:T(8,128)(2,1)} %get-tuple-element.602.expert_out_ref) | copy-start | bytes 25165828 | tf_op jit(solution)/shard_map/cond
  43.7 12.7 %copy-start.13 = (bf16[1024,2048]{1,0:T(8,128)(2,1)S(1)}, bf16[1024,2048]{1,0:T(8,128)(2,1)}, u32[]{:S(2)}) copy-start(bf16[1024,2048]{1,0:T(8,128)(2,1)} %get-tuple-element.599.dense_in_ref) | copy-start | bytes 12582916 | tf_op jit(solution)/shard_map/cond
  43.7 12.7 %copy-start.18 = (bf16[2048,1024]{1,0:T(8,128)(2,1)S(1)}, bf16[2048,1024]{1,0:T(8,128)(2,1)}, u32[]{:S(2)}) copy-start(bf16[2048,1024]{1,0:T(8,128)(2,1)} %get-tuple-element.600.dense_out_ref) | copy-start | bytes 12582916 | tf_op jit(solution)/shard_map/cond
  43.7 12.7 %copy-start.28 = (bf16[32,1024]{1,0:T(8,128)(2,1)S(1)}, bf16[32,1024]{1,0:T(8,128)(2,1)}, u32[]{:S(2)}) copy-start(bf16[32,1024]{1,0:T(8,128)(2,1)} %get-tuple-element.598.router_ref) | copy-start | bytes 196612 | tf_op jit(solution)/shard_map/cond
  73.5 3.3 %collective-permute-start.10 = (bf16[128,1024]{1,0:T(8,128)(2,1)S(1)}, bf16[128,1024]{1,0:T(8,128)(2,1)}, u32[]{:S(2)}, u32[]{:S(2)}) collective-permute-start(bf16[128,1024]{1,0:T(8,128)(2,1)S(1)} %get-tuple-element.984), channel_id=1, source_target_pairs={{0,16},{16,32},{32,48},{48,64},{64,80},{80,96},{96,112},{112,0},{1... | collective-permute-start | bytes 786440 | tf_op jit(solution)/shard_map/ppermute | solution.py:358
  73.6 3.2 %copy-start.25 = (bf16[1,1024,32]{1,2,0:T(8,128)(2,1)S(1)}, bf16[1,1024,32]{1,2,0:T(8,128)(2,1)}, u32[]{:S(2)}) copy-start(bf16[1,1024,32]{1,2,0:T(8,128)(2,1)} %param.31) | copy-start | bytes 196612
  77.8 12.7 %copy-start.4 = (bf16[2,1024,2048]{2,1,0:T(8,128)(2,1)S(1)}, bf16[2,1024,2048]{2,1,0:T(8,128)(2,1)}, u32[]{:S(2)}) copy-start(bf16[2,1024,2048]{2,1,0:T(8,128)(2,1)} %get-tuple-element.624.expert_in_ref) | copy-start | bytes 25165828 | tf_op jit(solution)/shard_map/while/body/eval_jaxpr/cond
  77.8 12.7 %copy-start.9 = (bf16[2,2048,1024]{2,1,0:T(8,128)(2,1)S(1)}, bf16[2,2048,1024]{2,1,0:T(8,128)(2,1)}, u32[]{:S(2)}) copy-start(bf16[2,2048,1024]{2,1,0:T(8,128)(2,1)} %get-tuple-element.625.expert_out_ref) | copy-start | bytes 25165828 | tf_op jit(solution)/shard_map/while/body/eval_jaxpr/cond
  77.8 12.7 %copy-start.14 = (bf16[1024,2048]{1,0:T(8,128)(2,1)S(1)}, bf16[1024,2048]{1,0:T(8,128)(2,1)}, u32[]{:S(2)}) copy-start(bf16[1024,2048]{1,0:T(8,128)(2,1)} %get-tuple-element.622.dense_in_ref) | copy-start | bytes 12582916 | tf_op jit(solution)/shard_map/while/body/eval_jaxpr/cond
  77.9 12.7 %copy-start.19 = (bf16[2048,1024]{1,0:T(8,128)(2,1)S(1)}, bf16[2048,1024]{1,0:T(8,128)(2,1)}, u32[]{:S(2)}) copy-start(bf16[2048,1024]{1,0:T(8,128)(2,1)} %get-tuple-element.623.dense_out_ref) | copy-start | bytes 12582916 | tf_op jit(solution)/shard_map/while/body/eval_jaxpr/cond
  106.5 6.5 %collective-permute-start.8 = (bf16[128,1024]{1,0:T(8,128)(2,1)S(1)}, bf16[128,1024]{1,0:T(8,128)(2,1)S(1)}, u32[]{:S(2)}, u32[]{:S(2)}) collective-permute-start(bf16[128,1024]{1,0:T(8,128)(2,1)S(1)} %param.14), channel_id=1, source_target_pairs={{0,32},{16,48},{32,64},{48,80},{64,96},{80,112},{96,0},{112,16},{1... | collective-permute-start | bytes 786440 | tf_op jit(solution)/shard_map/while/body/eval_jaxpr/cond/branch_1_fun/ppermute | solution.py:378
  114.8 60.1 %collective-permute-start.8 = (bf16[128,1024]{1,0:T(8,128)(2,1)S(1)}, bf16[128,1024]{1,0:T(8,128)(2,1)S(1)}, u32[]{:S(2)}, u32[]{:S(2)}) collective-permute-start(bf16[128,1024]{1,0:T(8,128)(2,1)S(1)} %param.14), channel_id=1, source_target_pairs={{0,32},{16,48},{32,64},{48,80},{64,96},{80,112},{96,0},{112,16},{1... | collective-permute-start | bytes 786440 | tf_op jit(solution)/shard_map/while/body/eval_jaxpr/cond/branch_1_fun/ppermute | solution.py:378
  176.7 6.5 %collective-permute-start.8 = (bf16[128,1024]{1,0:T(8,128)(2,1)S(1)}, bf16[128,1024]{1,0:T(8,128)(2,1)S(1)}, u32[]{:S(2)}, u32[]{:S(2)}) collective-permute-start(bf16[128,1024]{1,0:T(8,128)(2,1)S(1)} %param.14), channel_id=1, source_target_pairs={{0,32},{16,48},{32,64},{48,80},{64,96},{80,112},{96,0},{112,16},{1... | collective-permute-start | bytes 786440 | tf_op jit(solution)/shard_map/while/body/eval_jaxpr/cond/branch_1_fun/ppermute | solution.py:378
